TPU v7x, 32 devices: a whole 2x2x4 slice. The times are simulated.
32 devices in a mesh: groups: 1, tok: 32 (over z, y, x, core).
Axes of the slice: x: 2, y: 2, z: 4, core: 2. Of those that a mesh axis runs over, the one named last changes fastest.
Arguments:
- queries: bfloat16 [4096, 2560], P(('groups', 'tok')), may hold values from -5 to 5
- key_rows: bfloat16 [4096, 2560], P(('groups', 'tok')), may hold values from -5 to 5
- value_rows: bfloat16 [4096, 2560], P(('groups', 'tok')), may hold values from -6 to 6
- learn_rates: float32 [4096, 8], P(('groups', 'tok')), may hold values from 0.0002 to 0.002
- frame_order: int32 [4096], P('groups'), may hold values from 0 to 4095, as said below
- window_ids: int32 [4096], P('groups'), may hold values from 0 to 7, never falling along the last dimension, each value on 1 to 2048 neighbouring positions
- fast_init: bfloat16 [640, 3, 2560], replicated, may hold values from -0.3125 to 0.3125
- norm_gain: float32 [2560], replicated, may hold values from 0.5 to 1.5
Outputs:
- layer_out: bfloat16 [4096, 2560], P(('groups', 'tok'))
Inputs may be any that keep to these rules, and one draw needn't show every extreme that they name: frame_order[i] is the sequence position of the token stored at row i; every position appears once, and every aligned block of 128 stored rows holds exactly 4 positions of every aligned block of 128 positions.
All inputs are finite; a program needn't handle non-finite values.
Results may differ from a plain program's by a relative error of at most 0.025.
Values may be sent and summed in bfloat16 or wider, within the bound.
A program may use at most 192 MiB of HBM per device.

v0:
```python
import functools

import jax
import jax.numpy as jnp
from jax import lax
from jax.experimental import pallas as pl
from jax.experimental.pallas import tpu as pltpu
from jax.sharding import Mesh, PartitionSpec as P

HEADS = 8
ATT_DIM = 128
WINDOW = 1024
SPLIT = 4

epsilon = 1e-06
BF = jnp.bfloat16
F32 = jnp.float32
VM = pl.BlockSpec(memory_space=pltpu.VMEM)
NT = (((1,), (1,)), ((), ()))
TN = (((0,), (0,)), ((), ()))
VMEM_BYTES = 60 * 1024 * 1024


def dot_nt(a, b):
    return lax.dot_general(a, b, NT, preferred_element_type=F32)


def dot_tn(a, b):
    return lax.dot_general(a, b, TN, preferred_element_type=F32)


def dot_nn(a, b):
    return jnp.dot(a, b, preferred_element_type=F32)


def one_hot(left, right):
    return jnp.where(left == right, 1.0, 0.0).astype(BF)


def pack_kernel(home, rank_ref, wide_ref, own_ref, query_ref, key_ref, value_ref, out_ref):
    rank = rank_ref[...]
    wide = one_hot(wide_ref[...], rank)
    own = one_hot(own_ref[...], rank)
    groups, width = out_ref.shape[1], out_ref.shape[3]
    keys = dot_nn(wide, key_ref[...]).astype(BF)
    values = dot_nn(wide, value_ref[...]).astype(BF)
    rows = dot_nn(own, query_ref[...]).astype(BF)
    half = groups * home
    out_ref[0, :, 0:home, :] = keys[:half].reshape(groups, home, width)
    out_ref[0, :, home : 2 * home, :] = values[:half].reshape(groups, home, width)
    out_ref[0, :, 2 * home : 3 * home, :] = keys[half:].reshape(groups, home, width)
    out_ref[0, :, 3 * home : 4 * home, :] = values[half:].reshape(groups, home, width)
    out_ref[0, :, 4 * home :, :] = rows.reshape(groups, home, width)


def grads_kernel(home, head_dim, recv_ref, rate_ref, weight_ref, out_ref):
    count, _, width = recv_ref.shape
    tokens = count * home
    keys = recv_ref[:, 0:home, :].reshape(tokens, width)
    values = recv_ref[:, home : 2 * home, :].reshape(tokens, width).astype(F32)
    column = lax.broadcasted_iota(jnp.int32, (1, width), 1)
    for which in range(width // head_dim):
        inside = (column >= which * head_dim) & (column < (which + 1) * head_dim)
        key_part = jnp.where(inside, keys.astype(F32), 0.0).astype(BF)
        target = jnp.where(inside, values * rate_ref[:, which : which + 1], 0.0).astype(BF)
        gate = dot_nt(key_part, weight_ref[0])
        upward = dot_nt(key_part, weight_ref[1])
        backward = dot_nt(target, weight_ref[2])
        sigmoid = jax.nn.sigmoid(gate)
        active = gate * sigmoid
        product = (active * upward).astype(BF)
        delta_gate = (backward * upward * sigmoid * (1.0 + gate * (1.0 - sigmoid))).astype(BF)
        delta_upper = (backward * active).astype(BF)
        parts = (
            dot_tn(delta_gate, key_part),
            dot_tn(delta_upper, key_part),
            dot_tn(product, target),
        )
        for matrix, part in enumerate(parts):
            if which == 0:
                out_ref[matrix] = part.astype(BF)
            else:
                out_ref[matrix] = jnp.where(inside, part, out_ref[matrix].astype(F32)).astype(BF)


def attend_kernel(home, chunk, recv_ref, near_ref, kpos_ref, qpos_ref, low_ref, high_ref, begin_ref, out_ref, query_ref):
    count, _, width = recv_ref.shape
    tokens = count * home
    def block(ref, index):
        return ref[:, index * home : (index + 1) * home, :].reshape(tokens, width)

    keys = jnp.concatenate([block(recv_ref, 0), block(recv_ref, 2), block(near_ref, 0)], axis=0)
    values = jnp.concatenate([block(recv_ref, 1), block(recv_ref, 3), block(near_ref, 1)], axis=0)
    arrived = block(recv_ref, 4)
    kpos = kpos_ref[...]
    qpos = qpos_ref[...]
    for start in range(0, tokens, chunk):
        place = begin_ref[start : start + chunk, :]
        query = dot_nn(one_hot(place, qpos), arrived).astype(BF)
        query_ref[start : start + chunk, :] = query
        scores = dot_nt(query, keys) * ATT_DIM ** (-0.5)
        allowed = (kpos >= low_ref[start : start + chunk, :]) & (
            kpos < high_ref[start : start + chunk, :]
        )
        scores = jnp.where(allowed, scores, -1e30)
        peak = jnp.max(scores, axis=1, keepdims=True)
        weights = jnp.exp(scores - peak)
        total = jnp.sum(weights, axis=1, keepdims=True)
        out_ref[start : start + chunk, :] = dot_nn(weights.astype(BF), values) / total


def apply_kernel(head_dim, part_ref, query_ref, weight_ref, grad_ref, attended_ref, *rest):
    outs, held = rest[:-1], rest[-1]
    width = query_ref.shape[1]
    column = lax.broadcasted_iota(jnp.int32, (1, width), 1)
    insides = [
        (column >= which * head_dim) & (column < (which + 1) * head_dim)
        for which in range(width // head_dim)
    ]
    fresh = []
    for matrix in range(3):
        base = weight_ref[matrix].astype(F32)
        update = base + grad_ref[matrix].astype(F32)
        base_square = base * base
        update_square = update * update
        scaling = jnp.zeros_like(update)
        for inside in insides:
            old = jnp.sum(jnp.where(inside, base_square, 0.0), axis=1, keepdims=True)
            new = jnp.sum(jnp.where(inside, update_square, 0.0), axis=1, keepdims=True)
            ratio = jnp.sqrt(old + epsilon) / jnp.sqrt(new + epsilon)
            scaling = jnp.where(inside, ratio, scaling)
        fresh.append((update * scaling).astype(BF))
    query = query_ref[...].astype(F32)
    result = attended_ref[...]
    for inside in insides:
        query_part = jnp.where(inside, query, 0.0).astype(BF)
        gate = dot_nt(query_part, fresh[0])
        upward = dot_nt(query_part, fresh[1])
        product = (gate * jax.nn.sigmoid(gate) * upward).astype(BF)
        result = result + jnp.where(inside, dot_nn(product, fresh[2]), 0.0)
    held[...] = result
    count = len(outs)
    rows = held.shape[0] // count
    for step, out_ref in enumerate(outs):
        target = lax.rem(part_ref[0] + step, count)
        out_ref[...] = held[pl.ds(pl.multiple_of(target * rows, rows), rows), :].astype(BF)


def norm_kernel(place_ref, gain_ref, *rest):
    parts, out_ref = rest[:-1], rest[-1]
    count = len(parts)
    width = parts[0].shape[1]
    square = 0.0
    for part_ref in parts:
        part = part_ref[...].astype(F32)
        square = square + jnp.sum(part * part, axis=1, keepdims=True)
    scale = lax.rsqrt(square / (count * width) + epsilon)
    for step, part_ref in enumerate(parts):
        source = lax.rem(place_ref[0] - step + count, count)
        columns = pl.ds(pl.multiple_of(source * width, width), width)
        out_ref[:, columns] = (
            part_ref[...].astype(F32) * scale * gain_ref[:, columns]
        ).astype(BF)


def call(kernel, name, out_shape, flops, size, **options):
    return pl.pallas_call(
        kernel,
        name=name,
        out_shape=out_shape,
        compiler_params=pltpu.CompilerParams(vmem_limit_bytes=VMEM_BYTES),
        cost_estimate=pl.CostEstimate(flops=flops, bytes_accessed=size, transcendentals=0),
        **options,
    )


def shards(
    queries, key_rows, value_rows, learn_rates, frame_order, window_ids, fast_init, norm_gain
):
    tok_dev, model = queries.shape
    groups = lax.axis_size("seg")
    sections = groups * SPLIT
    group = lax.axis_index("seg")
    part = lax.axis_index("hd")
    rank_own = part * groups + group
    slots = tok_dev // sections
    half = WINDOW // 2
    home = SPLIT * slots
    reach = -(-half // tok_dev) * slots
    assert reach == home and groups % 2 == 0
    width = model // SPLIT
    head_dim = model // HEADS
    hidden = fast_init.shape[0]
    tokens = sections * home
    counter = jnp.arange(tok_dev, dtype=jnp.int32)

    order = frame_order.reshape(sections, tok_dev)
    sort_key = order // tok_dev * tok_dev + counter[None, :]
    ranks = jnp.sum(
        (sort_key[:, None, :] < sort_key[:, :, None]).astype(jnp.int32), axis=2
    )
    own_rank = lax.dynamic_slice_in_dim(ranks, rank_own, 1, 0)

    every = jnp.arange(groups, dtype=jnp.int32)
    inner = jnp.arange(home, dtype=jnp.int32)
    outer = every + 2 * (every % 2) - 1
    wide_want = (
        jnp.concatenate([every, outer])[:, None] * home + inner[None, :]
    ).reshape(-1, 1)
    rows = 5 * home
    send = call(
        functools.partial(pack_kernel, home),
        "pack",
        jax.ShapeDtypeStruct((SPLIT, groups, rows, width), BF),
        10 * tok_dev * tok_dev * model,
        2 * model * (3 * tok_dev + groups * rows),
        grid=(SPLIT,),
        in_specs=[
            pl.BlockSpec((1, tok_dev), lambda h: (0, 0)),
            pl.BlockSpec((2 * groups * home, 1), lambda h: (0, 0)),
            pl.BlockSpec((tok_dev, 1), lambda h: (0, 0)),
            pl.BlockSpec((tok_dev, width), lambda h: (0, h)),
            pl.BlockSpec((tok_dev, width), lambda h: (0, h)),
            pl.BlockSpec((tok_dev, width), lambda h: (0, h)),
        ],
        out_specs=pl.BlockSpec((1, groups, rows, width), lambda h: (h, 0, 0, 0)),
    )(own_rank, wide_want, counter[:, None], queries, key_rows, value_rows)
    recv = lax.all_to_all(
        send.reshape(sections, rows, width),
        ("hd", "seg"),
        split_axis=0,
        concat_axis=0,
        tiled=True,
    )
    near = lax.ppermute(recv[:, : 2 * home], "seg", [(i, i ^ 1) for i in range(groups)])

    sorting = (own_rank == counter[:, None]).astype(F32)
    rates = jnp.dot(sorting, learn_rates, precision=lax.Precision.HIGHEST)
    rates = rates.reshape(groups, home, SPLIT, HEADS // SPLIT).transpose(2, 0, 1, 3)
    rates = lax.all_to_all(
        rates.reshape(sections, home, HEADS // SPLIT),
        ("hd", "seg"),
        split_axis=0,
        concat_axis=0,
        tiled=True,
    ).reshape(tokens, HEADS // SPLIT)

    odd = group % 2
    held_groups = jnp.stack([group, group + 2 * odd - 1, group + 1 - 2 * odd])
    wanted = (held_groups[:, None] * home + inner[None, :]).reshape(-1)
    match = ranks[:, None, :] == wanted[None, :, None]
    positions = jnp.max(jnp.where(match, order[:, None, :], -1), axis=2)
    kpos = positions.reshape(sections, 3, home).transpose(1, 0, 2).reshape(1, 3 * tokens)
    qpos = kpos[:, :tokens]
    first = group * tokens
    place = first + jnp.arange(tokens, dtype=jnp.int32)
    ids = lax.dynamic_slice_in_dim(window_ids, first, tokens, 0)
    clip_low = jnp.sum((window_ids[None, :] < ids[:, None]).astype(jnp.int32), axis=1)
    clip_high = jnp.sum((window_ids[None, :] <= ids[:, None]).astype(jnp.int32), axis=1)
    low = jnp.maximum(clip_low, place - (half - 1))[:, None]
    high = jnp.minimum(clip_high, place + half)[:, None]

    weight = lax.dynamic_slice_in_dim(fast_init, part * width, width, 2).transpose(1, 0, 2)
    grads = call(
        functools.partial(grads_kernel, home, head_dim),
        "grads",
        jax.ShapeDtypeStruct((3, hidden, width), BF),
        24 * tokens * hidden * width,
        4 * tokens * width + 12 * hidden * width,
        in_specs=[VM] * 3,
        out_specs=VM,
    )(recv, rates, weight)
    grads = lax.psum(grads, "seg")

    whole = lambda h: (0, 0)
    attended, query_seq = call(
        functools.partial(attend_kernel, home, min(tokens, 128)),
        "attend",
        (
            jax.ShapeDtypeStruct((tokens, width), F32),
            jax.ShapeDtypeStruct((tokens, width), BF),
        ),
        24 * tokens * tokens * width,
        20 * tokens * width,
        grid=(width // ATT_DIM,),
        in_specs=[
            pl.BlockSpec((sections, rows, ATT_DIM), lambda h: (0, 0, h)),
            pl.BlockSpec((sections, 2 * home, ATT_DIM), lambda h: (0, 0, h)),
            pl.BlockSpec((1, 3 * tokens), whole),
            pl.BlockSpec((1, tokens), whole),
            pl.BlockSpec((tokens, 1), whole),
            pl.BlockSpec((tokens, 1), whole),
            pl.BlockSpec((tokens, 1), whole),
        ],
        out_specs=(
            pl.BlockSpec((tokens, ATT_DIM), lambda h: (0, h)),
            pl.BlockSpec((tokens, ATT_DIM), lambda h: (0, h)),
        ),
    )(recv, near, kpos, qpos, low, high, place[:, None])

    scalar = pl.BlockSpec(memory_space=pltpu.SMEM)
    pieces = call(
        functools.partial(apply_kernel, head_dim),
        "apply",
        tuple(jax.ShapeDtypeStruct((tok_dev, width), BF) for _ in range(SPLIT)),
        12 * tokens * hidden * width,
        8 * tokens * width + 12 * hidden * width,
        in_specs=[scalar] + [VM] * 4,
        out_specs=(VM,) * SPLIT,
        scratch_shapes=[pltpu.VMEM((tokens, width), F32)],
    )(part[None], query_seq, weight, grads, attended)
    returned = [
        lax.ppermute(
            piece,
            ("hd", "seg"),
            [
                (h * groups + g, g * SPLIT + (h + step) % SPLIT)
                for h in range(SPLIT)
                for g in range(groups)
            ],
        )
        for step, piece in enumerate(pieces)
    ]
    return call(
        norm_kernel,
        "norm",
        jax.ShapeDtypeStruct((tok_dev, model), BF),
        8 * tok_dev * model,
        4 * tok_dev * model,
        in_specs=[scalar] + [VM] * (1 + SPLIT),
        out_specs=VM,
    )((rank_own % SPLIT)[None], norm_gain[None, :], *returned)


def solution(mesh):
    count = mesh.shape["tok"]
    split_mesh = Mesh(
        mesh.devices.reshape(mesh.shape["groups"], SPLIT, count // SPLIT),
        ("groups", "hd", "seg"),
    )
    rows = P(("groups", "hd", "seg"), None)
    return jax.shard_map(
        shards,
        mesh=split_mesh,
        in_specs=(rows, rows, rows, rows, P("groups"), P("groups"), P(), P()),
        out_specs=rows,
        check_vma=False,
    )
```

profile of v0, /device:TPU:0, one launch (start us, length us, event | category | flops | bytes accessed | tf_op | source)
XLA Modules:
  0.0 247.3 jit_solution(1161413009054542273)
XLA Ops:
  6.5 0.7 fusion.4
  7.3 1.3 convert_reduce_fusion.2
  8.6 0.1 fusion
  8.7 0.1 reshape.203
  8.8 0.7 copy.34
  9.5 7.3 %all-to-all-start.1 = ((f32[32,16,2]{1,2,0:T(2,128)}), f32[32,16,2]{1,2,0:T(2,128)S(1)}, u32[]{:S(2)}, u32[]{:S(2)}) async-start(f32[32,16,2]{1,2,0:T(2,128)} %bitcast.14), calls=%async_computation.1 | async-start | bytes 65536 | tf_op jit(solution)/shard_map/all_to_all | solution.py:240
  16.8 0.5 constant_dynamic-slice_fusion.rank_ref
  17.4 0.1 add_multiply_fusion
  17.4 0.1 iota_add_fusion.1
  17.5 0.8 add.178.wide_ref
  18.3 0.6 iota.38.own_ref
  18.9 5.0 %pack.1 = bf16[4,8,80,640]{3,2,1,0:T(8,128)(2,1)} custom-call(s32[1,128]{1,0:T(1,128)} %constant_dynamic-slice_fusion.rank_ref, s32[256,1]{1,0:T(8,128)} %add.178.wide_ref, s32[128,1]{1,0:T(8,128)} %iota.38.own_ref, bf16[128,2560]{1,0:T(8,128)(2,1)} %query_ref.1, bf16[128,2560]{1,0:T(8,128)(2,1)} %key_ref.1, bf16[128,2560]{1,0:T(8,128)(2,1)} %value_ref.1), custom_call_target="tpu_custom_call" | custom-call | flops 419430400 | bytes 5242880 | tf_op jit(solution)/shard_map/pack/pallas_call | solution.py:211
  23.9 0.2 all-to-all-done.1
  24.1 5.7 %all-to-all-start = ((bf16[32,80,640]{2,1,0:T(8,128)(2,1)}), bf16[32,80,640]{2,1,0:T(8,128)(2,1)S(1)}, u32[]{:S(2)}, u32[]{:S(2)}) async-start(bf16[32,80,640]{2,1,0:T(8,128)(2,1)} %bitcast.23), calls=%async_computation | async-start | bytes 6553600 | tf_op jit(solution)/shard_map/all_to_all | solution.py:228
  29.8 0.1 add_multiply_fusion.1
  29.9 3.4 %dynamic-slice_bitcast_fusion.weight_ref = bf16[3,640,640]{2,1,0:T(8,128)(2,1)} fusion(bf16[640,3,2560]{2,0,1:T(8,128)(2,1)} %param.14, s32[]{:T(128)S(6)} %select_n.52), kind=kLoop, calls=%fused_computation.2 | loop fusion | bytes 4915204 | tf_op jit(solution)/shard_map/transpose | solution.py:263
  33.3 1.0 copy.35
  34.2 69.7 %all-to-all-done.recv_ref = bf16[32,80,640]{2,1,0:T(8,128)(2,1)S(1)} async-done(((bf16[32,80,640]{2,1,0:T(8,128)(2,1)}), bf16[32,80,640]{2,1,0:T(8,128)(2,1)S(1)}, u32[]{:S(2)}, u32[]{:S(2)}) %all-to-all-start) | async-done | bytes 3276832 | tf_op jit(solution)/shard_map/all_to_all | solution.py:228
  103.9 1.3 slice.8
  105.2 0.8 copy-done.1
  105.9 11.6 %grads.1 = bf16[3,640,640]{2,1,0:T(8,128)(2,1)} custom-call(bf16[32,80,640]{2,1,0:T(8,128)(2,1)} %copy-done.1, f32[512,2]{1,0:T(8,128)} %bitcast.24, bf16[3,640,640]{2,1,0:T(8,128)(2,1)} %dynamic-slice_bitcast_fusion.weight_ref), custom_call_target="tpu_custom_call" | custom-call | flops 5033164800 | bytes 6225920 | tf_op jit(solution)/shard_map/grads/pallas_call | solution.py:264
  117.6 0.1 iota_add_fusion.2
  117.6 0.1 add.171
  117.7 0.5 copy-done.6
  118.3 0.7 select_reduce_fusion
  118.9 0.1 copy.29
  119.0 0.1 copy.30
  119.1 0.1 reshape.202.kpos_ref
  119.2 0.6 slice.9.qpos_ref
  119.8 0.1 dynamic_slice.10
  119.9 2.0 convert_reduce_fusion
  121.9 0.2 copy.32
  122.0 0.1 copy.33
  122.2 0.7 iota_add_fusion.begin_ref
  122.9 0.9 add_minimum_fusion
  123.8 15.6 %attend.1 = (f32[512,640]{1,0:T(8,128)}, bf16[512,640]{1,0:T(8,128)(2,1)}) custom-call(bf16[32,80,640]{2,1,0:T(8,128)(2,1)} %copy-done.1, bf16[32,32,640]{2,1,0:T(8,128)(2,1)} %collective-permute-done.near_ref, s32[1,1536]{1,0:T(1,128)} %copy-done.8, s32[1,512]{1,0:T(1,128)} %slice.9.qpos_ref, s32[512,1]{1,0:T(8,128)} %get-tuple-element.20.low_ref, ...), custom_call_target="tpu_custom_call" | custom-call | flops 4026531840 | bytes 6553600 | tf_op jit(solution)/shard_map/attend/pallas_call | solution.py:276
  139.4 41.4 %all-reduce.2.cloned.1.call-done.grad_ref = bf16[3,640,640]{2,1,0:T(8,128)(2,1)} async-done(((bf16[3,640,640]{2,1,0:T(8,128)(2,1)}), bf16[3,640,640]{2,1,0:T(8,128)(2,1)}) %all-reduce.2.cloned.1.call-update) | async-done | bytes 2457616 | tf_op jit(solution)/shard_map/psum | solution.py:273
  180.8 9.9 %apply.1 = (bf16[128,640]{1,0:T(8,128)(2,1)}, bf16[128,640]{1,0:T(8,128)(2,1)}, bf16[128,640]{1,0:T(8,128)(2,1)}, bf16[128,640]{1,0:T(8,128)(2,1)}) custom-call(s32[1]{0:T(128)} %bitcast.1.part_ref, bf16[512,640]{1,0:T(8,128)(2,1)} %get-tuple-element.11.query_ref, bf16[3,640,640]{2,1,0:T(8,128)(2,1)} %dynamic-slice_bitcast_fusion.weight_ref, ...), custom_call_target="tpu_custom_call" | custom-call | flops 2516582400 | bytes 7536640 | tf_op jit(solution)/shard_map/apply/pallas_call | solution.py:302
  190.7 1.6 collective-permute-start.1
  192.3 3.1 %collective-permute-start.2 = (bf16[128,640]{1,0:T(8,128)(2,1)}, bf16[128,640]{1,0:T(8,128)(2,1)S(1)}, u32[]{:S(2)}, u32[]{:S(2)}) collective-permute-start(bf16[128,640]{1,0:T(8,128)(2,1)} %get-tuple-element.14), channel_id=1, source_target_pairs={{0,1},{1,5},{2,9},{3,13},{4,17},{5,21},{6,25},{7,29},{8,2},{9,6},{... | collective-permute-start | bytes 491528 | tf_op jit(solution)/shard_map/ppermute | solution.py:313
  195.4 2.2 collective-permute-start.3
  197.6 4.3 %collective-permute-start.4 = (bf16[128,640]{1,0:T(8,128)(2,1)}, bf16[128,640]{1,0:T(8,128)(2,1)S(1)}, u32[]{:S(2)}, u32[]{:S(2)}) collective-permute-start(bf16[128,640]{1,0:T(8,128)(2,1)} %get-tuple-element.16), channel_id=1, source_target_pairs={{0,3},{1,7},{2,11},{3,15},{4,19},{5,23},{6,27},{7,31},{8,0},{9,4},... | collective-permute-start | bytes 491528 | tf_op jit(solution)/shard_map/ppermute | solution.py:313
  201.9 0.6 broadcast_in_dim.19.gain_ref
  202.5 0.1 collective-permute-done.2.rest_1_
  202.6 19.3 %collective-permute-done.3.rest_2_ = bf16[128,640]{1,0:T(8,128)(2,1)S(1)} collective-permute-done((bf16[128,640]{1,0:T(8,128)(2,1)}, bf16[128,640]{1,0:T(8,128)(2,1)S(1)}, u32[]{:S(2)}, u32[]{:S(2)}) %collective-permute-start.3) | collective-permute-done | bytes 163872 | tf_op jit(solution)/shard_map/ppermute | solution.py:313
  221.9 15.6 %collective-permute-done.4.rest_3_ = bf16[128,640]{1,0:T(8,128)(2,1)S(1)} collective-permute-done((bf16[128,640]{1,0:T(8,128)(2,1)}, bf16[128,640]{1,0:T(8,128)(2,1)S(1)}, u32[]{:S(2)}, u32[]{:S(2)}) %collective-permute-start.4) | collective-permute-done | bytes 163872 | tf_op jit(solution)/shard_map/ppermute | solution.py:313
  237.5 0.6 copy-done.5
  238.1 2.3 norm.1
  (25 shorter events, 0.1 us)
Async XLA Ops:
  6.5 2.1 copy-start
  9.5 14.6 %all-to-all-start.1 = ((f32[32,16,2]{1,2,0:T(2,128)}), f32[32,16,2]{1,2,0:T(2,128)S(1)}, u32[]{:S(2)}, u32[]{:S(2)}) async-start(f32[32,16,2]{1,2,0:T(2,128)} %bitcast.14), calls=%async_computation.1 | async-start | bytes 65536 | tf_op jit(solution)/shard_map/all_to_all | solution.py:240
  24.1 79.8 %all-to-all-start = ((bf16[32,80,640]{2,1,0:T(8,128)(2,1)}), bf16[32,80,640]{2,1,0:T(8,128)(2,1)S(1)}, u32[]{:S(2)}, u32[]{:S(2)}) async-start(bf16[32,80,640]{2,1,0:T(8,128)(2,1)} %bitcast.23), calls=%async_computation | async-start | bytes 6553600 | tf_op jit(solution)/shard_map/all_to_all | solution.py:228
  29.7 151.1 %all-reduce.2.cloned.1.call-start = ((), (), s32[]{:S(2)}) async-start(), calls=%async_computation.2 | async-start | bytes 4915200 | tf_op jit(solution)/shard_map/psum | solution.py:273
  103.9 2.1 copy-start.1
  105.2 18.6 %collective-permute-start = (bf16[32,32,640]{2,1,0:T(8,128)(2,1)}, bf16[32,32,640]{2,1,0:T(8,128)(2,1)}, u32[]{:S(2)}, u32[]{:S(2)}) collective-permute-start(bf16[32,32,640]{2,1,0:T(8,128)(2,1)} %slice.8), channel_id=1, source_target_pairs={{0,1},{1,0},{2,3},{3,2},{4,5},{5,4},{6,7},{7,6},{8,9},{9,8},{10,11... | collective-permute-start | bytes 3932168 | tf_op jit(solution)/shard_map/ppermute | solution.py:235
  117.5 0.7 copy-start.6
  117.5 2.3 copy-start.9
  119.2 4.6 %copy-start.8 = (s32[1,1536]{1,0:T(1,128)}, s32[1,1536]{1,0:T(1,128)S(1)}, u32[]{:S(2)}) copy-start(s32[1,1536]{1,0:T(1,128)S(1)} %reshape.202.kpos_ref) | copy-start | bytes 18436
  180.8 21.1 %copy-start.7 = (f32[2560]{0:T(1024)S(1)}, f32[2560]{0:T(1024)}, u32[]{:S(2)}) copy-start(f32[2560]{0:T(1024)} %param.15) | copy-start | bytes 30724
  190.7 11.7 %collective-permute-start.1 = (bf16[128,640]{1,0:T(8,128)(2,1)}, bf16[128,640]{1,0:T(8,128)(2,1)S(1)}, u32[]{:S(2)}, u32[]{:S(2)}) collective-permute-start(bf16[128,640]{1,0:T(8,128)(2,1)} %get-tuple-element.13), channel_id=1, source_target_pairs={{0,0},{1,4},{2,8},{3,12},{4,16},{5,20},{6,24},{7,28},{8,1},{9,5},{... | collective-permute-start | bytes 491528 | tf_op jit(solution)/shard_map/ppermute | solution.py:313
  192.3 10.3 %collective-permute-start.2 = (bf16[128,640]{1,0:T(8,128)(2,1)}, bf16[128,640]{1,0:T(8,128)(2,1)S(1)}, u32[]{:S(2)}, u32[]{:S(2)}) collective-permute-start(bf16[128,640]{1,0:T(8,128)(2,1)} %get-tuple-element.14), channel_id=1, source_target_pairs={{0,1},{1,5},{2,9},{3,13},{4,17},{5,21},{6,25},{7,29},{8,2},{9,6},{... | collective-permute-start | bytes 491528 | tf_op jit(solution)/shard_map/ppermute | solution.py:313
  195.4 26.5 %collective-permute-start.3 = (bf16[128,640]{1,0:T(8,128)(2,1)}, bf16[128,640]{1,0:T(8,128)(2,1)S(1)}, u32[]{:S(2)}, u32[]{:S(2)}) collective-permute-start(bf16[128,640]{1,0:T(8,128)(2,1)} %get-tuple-element.15), channel_id=1, source_target_pairs={{0,2},{1,6},{2,10},{3,14},{4,18},{5,22},{6,26},{7,30},{8,3},{9,7},... | collective-permute-start | bytes 491528 | tf_op jit(solution)/shard_map/ppermute | solution.py:313
  197.6 39.9 %collective-permute-start.4 = (bf16[128,640]{1,0:T(8,128)(2,1)}, bf16[128,640]{1,0:T(8,128)(2,1)S(1)}, u32[]{:S(2)}, u32[]{:S(2)}) collective-permute-start(bf16[128,640]{1,0:T(8,128)(2,1)} %get-tuple-element.16), channel_id=1, source_target_pairs={{0,3},{1,7},{2,11},{3,15},{4,19},{5,23},{6,27},{7,31},{8,0},{9,4},... | collective-permute-start | bytes 491528 | tf_op jit(solution)/shard_map/ppermute | solution.py:313
  202.5 35.0 %copy-start.2 = (bf16[128,640]{1,0:T(8,128)(2,1)}, bf16[128,640]{1,0:T(8,128)(2,1)S(1)}, u32[]{:S(2)}) copy-start(bf16[128,640]{1,0:T(8,128)(2,1)S(1)} %collective-permute-done.1.rest_0_) | copy-start | bytes 491524
  202.6 34.9 %copy-start.3 = (bf16[128,640]{1,0:T(8,128)(2,1)}, bf16[128,640]{1,0:T(8,128)(2,1)S(1)}, u32[]{:S(2)}) copy-start(bf16[128,640]{1,0:T(8,128)(2,1)S(1)} %collective-permute-done.2.rest_1_) | copy-start | bytes 491524
  221.9 15.6 %copy-start.4 = (bf16[128,640]{1,0:T(8,128)(2,1)}, bf16[128,640]{1,0:T(8,128)(2,1)S(1)}, u32[]{:S(2)}) copy-start(bf16[128,640]{1,0:T(8,128)(2,1)S(1)} %collective-permute-done.3.rest_2_) | copy-start | bytes 491524
  237.5 0.7 copy-start.5
Sparse Core Ops, SparseCore 0:
  117.7 63.0 all-reduce.1
where the time goes:
time: 248 us; the launch traced here: 247 us
  waiting for transfers between devices  146 us (59%)
  Pallas kernels  44.4 us (18%)
  starting transfers between devices  24.1 us (10%)
  between operations  13.6 us (5%)
  local copies, waits for them, and re-layouts  12.2 us (5%)
  other arithmetic  6.61 us (3%)
    all_to_all x1, waiting for transfers between devices, shards(): lax.all_to_all(send.reshape(sections, rows, width), ('hd', 'seg'), split_...  69.7 us
    psum x1, waiting for transfers between devices, shards(): grads = lax.psum(grads, 'seg')  41.4 us
    ppermute x4, waiting for transfers between devices, shards(): lax.ppermute(piece, ('hd', 'seg'), [(h * groups + g, g * SPLIT + (h + ste...  35 us
    pallas_call x1, Pallas kernels, shards(): call(functools.partial(attend_kernel, home, min(tokens, 128)), 'attend',...  15.6 us
    pallas_call x1, Pallas kernels, shards(): call(functools.partial(grads_kernel, home, head_dim), 'grads', jax.ShapeD...  11.6 us
    ppermute x4, starting transfers between devices, shards(): lax.ppermute(piece, ('hd', 'seg'), [(h * groups + g, g * SPLIT + (h + ste...  11.1 us
    pallas_call x1, Pallas kernels, shards(): call(functools.partial(apply_kernel, head_dim), 'apply', tuple((jax.Shape...  9.93 us
    all_to_all x1, starting transfers between devices, shards(): lax.all_to_all(rates.reshape(sections, home, HEADS // SPLIT), ('hd', 'seg...  7.33 us
  transfers between devices with their start and end apart: 8, of which 6 were waited for; matrix products, arithmetic and copies ran while one was open for 5% of the time, Pallas kernels for 13%

commit v1 on v0

v1 whole, which is shorter than its diff:
```python
import functools

import jax
import jax.numpy as jnp
from jax import lax
from jax.experimental import pallas as pl
from jax.experimental.pallas import tpu as pltpu
from jax.sharding import PartitionSpec as P

HEADS = 8
ATT_DIM = 128
WINDOW = 1024
SPLIT = 4

epsilon = 1e-06
BF = jnp.bfloat16
F32 = jnp.float32
I32 = jnp.int32
LANES = 128
VM = pl.BlockSpec(memory_space=pltpu.VMEM)
ANY = pl.BlockSpec(memory_space=pl.ANY)
NT = (((1,), (1,)), ((), ()))
TN = (((0,), (0,)), ((), ()))
VMEM_BYTES = 62 * 1024 * 1024


def dot_nt(a, b):
    return lax.dot_general(a, b, NT, preferred_element_type=F32)


def dot_tn(a, b):
    return lax.dot_general(a, b, TN, preferred_element_type=F32)


def dot_nn(a, b):
    return jnp.dot(a, b, preferred_element_type=F32)


def iota(shape, dim):
    return lax.broadcasted_iota(I32, shape, dim)


class Place:
    def __init__(self, count):
        self.count = count
        self.segs = count // SPLIT
        self.chips = self.segs // 2

    def shift(self, hd):
        return ((hd % 2) * 2 + hd // 2) % self.chips

    def seg(self, hd, within):
        chip, core = within // 2, within % 2
        if self.chips == 4:
            step = 2 * (chip // 2) + (chip % 2 + chip // 2) % 2
        else:
            step = chip
        return (step - self.shift(hd) + self.chips) % self.chips * 2 + core

    def rank(self, hd, seg):
        pair, core = seg // 2, seg % 2
        step = (pair + self.shift(hd)) % self.chips
        if self.chips == 4:
            chip = 2 * (step // 2) + (step + step // 2) % 2
        else:
            chip = step
        return hd * self.segs + chip * 2 + core


def pack_kernel(segs, order_ref, rate_ref, query_ref, key_ref, value_ref, kv_ref, q_ref, small_ref):
    me = lax.axis_index("tok")
    tokens, width = key_ref.shape
    home = tokens // segs
    row = order_ref[pl.ds(me, 1), :].astype(F32)
    down, across = iota((tokens, tokens), 0), iota((tokens, tokens), 1)
    same = down == across
    column = jnp.sum(jnp.where(same, row, 0.0), axis=1, keepdims=True)
    span = 1.0 / (SPLIT * tokens)

    def sort_key(place, index):
        return jnp.floor((place + 0.5) * span) * tokens + index.astype(F32)

    key_row = sort_key(row, iota((1, tokens), 1))
    key_column = sort_key(column, iota((tokens, 1), 0))
    rank_row = jnp.sum(jnp.where(key_column < key_row, 1.0, 0.0), axis=0, keepdims=True)
    rank_column = jnp.sum(jnp.where(key_row < key_column, 1.0, 0.0), axis=1, keepdims=True)
    pick = jnp.where(down.astype(F32) == rank_row, 1.0, 0.0).astype(BF)
    keys = dot_nn(pick, key_ref[...]).astype(BF)
    values = dot_nn(pick, value_ref[...]).astype(BF)
    rows = dot_nn(pick, query_ref[...]).astype(BF)
    kv_ref[0, :, 0:home, :] = keys.reshape(segs, home, width)
    kv_ref[0, :, home : 2 * home, :] = values.reshape(segs, home, width)
    q_ref[0] = rows.reshape(segs, home, width)

    @pl.when(pl.program_id(0) == 0)
    def _():
        put = jnp.where(across.astype(F32) == rank_column, 1.0, 0.0)
        place = jnp.sum(put * column, axis=0, keepdims=True)
        rates = jnp.dot(rate_ref[...], put, precision=lax.Precision.HIGHEST)
        heads = HEADS // SPLIT
        for hd in range(SPLIT):
            small_ref[hd, 0:heads, :] = rates[hd * heads : (hd + 1) * heads]
            small_ref[hd, heads : heads + 1, :] = place
            small_ref[hd, heads + 1 :, :] = jnp.zeros_like(small_ref[hd, heads + 1 :, :])


def layer_kernel(
    place, head_dim, kv_ref, q_ref, small_ref, ids_ref, init_ref, gain_ref, out_ref,
    kv, queries, small, weight, total, part, half_in, half, slices, fresh, ahead, sorted_q,
    bias, combined, outgoing, returned,
    init_sem, kv_send, kv_recv, q_send, q_recv, small_send, small_recv, next_send, next_recv,
    prev_send, prev_recv, core_send, core_recv, cut_send, cut_recv, share_send, share_recv,
    pass_send, pass_recv, back_send, back_recv,
):
    me = lax.axis_index("tok")
    count, segs, chips = place.count, place.segs, place.chips
    hd, within = me // segs, me % segs
    chip, core = within // 2, within % 2
    seg = place.seg(hd, within)
    home, width = queries.shape[1], queries.shape[2]
    tokens = count * home
    hidden = weight.shape[1]
    side = hidden // 2
    rows = side // chips
    heads = width // head_dim
    partner = me + 1 - 2 * core
    after = place.rank(hd, (seg + 1) % segs)
    before = place.rank(hd, (seg + segs - 1) % segs)

    def remote(src, dst, send, recv, device):
        return pltpu.make_async_remote_copy(
            src_ref=src, dst_ref=dst, send_sem=send, recv_sem=recv,
            device_id={"tok": device}, device_id_type=pl.DeviceIdType.MESH,
        )

    def wait_all(buffer, sem):
        pltpu.make_async_copy(buffer, buffer, sem).wait()

    columns = pl.ds(pl.multiple_of(hd * width, LANES), width)
    load = pltpu.make_async_copy(init_ref.at[:, :, columns], weight, init_sem)
    load.start()

    barrier = pltpu.get_barrier_semaphore()

    def greet(step, carry):
        pl.semaphore_signal(
            barrier, inc=1, device_id={"tok": (me + step) % count},
            device_id_type=pl.DeviceIdType.MESH,
        )
        return carry

    lax.fori_loop(1, count, greet, 0)
    pl.semaphore_wait(barrier, count - 1)

    planes = [(hd + 2) % 4, 3 - hd, hd + 1 - 2 * (hd % 2), hd]

    def send_rows(plane, first):
        def body(step, carry):
            spot = (within + step) % segs
            there = plane * segs + spot
            where = place.seg(plane, spot)
            remote(small_ref.at[plane], small.at[me], small_send, small_recv, there).start()
            remote(kv_ref.at[plane, where], kv.at[1, me], kv_send, kv_recv.at[me], there).start()
            return carry

        lax.fori_loop(first, segs, body, 0)

    def send_queries(plane, first):
        def body(step, carry):
            spot = (within + step) % segs
            there = plane * segs + spot
            where = place.seg(plane, spot)
            remote(q_ref.at[plane, where], queries.at[me], q_send, q_recv, there).start()
            return carry

        lax.fori_loop(first, segs, body, 0)

    for order, plane in enumerate(planes):
        send_rows(plane, 1 if order == 3 else 0)

    def forward(block, source):
        remote(block, kv.at[0, source], next_send, next_recv, after).start()
        remote(block, kv.at[2, source], prev_send, prev_recv, before).start()

    own = kv_ref.at[hd, seg]
    forward(own, me)
    kv[1, me] = kv_ref[hd, seg]
    queries[me] = q_ref[hd, seg]
    small[me] = small_ref[hd]

    def arrive(plane, first):
        def body(step, carry):
            source = plane * segs + (within + segs - step) % segs
            block = kv.at[1, source]
            remote(block, block, kv_send, kv_recv.at[source], source).wait_recv()
            forward(block, source)
            return carry

        lax.fori_loop(first, segs, body, 0)

    total[...] = jnp.zeros_like(total)

    column = iota((1, width), 1)

    def span(which):
        low = which * head_dim // LANES * LANES
        high = -(-(which + 1) * head_dim // LANES) * LANES
        inside = (column[:, low:high] >= which * head_dim) & (
            column[:, low:high] < (which + 1) * head_dim
        )
        return slice(low, high), inside

    def pick_column(index, base, sources, which):
        lane = iota((home, LANES), 1) == index * home + iota((home, LANES), 0)
        held = small[pl.ds(base, sources), which, :]
        chosen = jnp.where(lane[None], held[:, None, :], 0.0)
        return jnp.sum(chosen, axis=2, keepdims=True).reshape(sources * home, 1)

    def learn(base, sources):
        group = sources * home
        for which in range(heads):
            lanes, inside = span(which)
            keys = kv[1, pl.ds(base, sources), 0:home, lanes].reshape(group, -1)
            values = kv[1, pl.ds(base, sources), home : 2 * home, lanes].reshape(group, -1)
            rate = pick_column(seg, base, sources, which)
            key_part = jnp.where(inside, keys.astype(F32), 0.0).astype(BF)
            target = jnp.where(inside, values.astype(F32) * rate, 0.0).astype(BF)
            gate = dot_nt(key_part, weight[0, :, lanes])
            upward = dot_nt(key_part, weight[1, :, lanes])
            backward = dot_nt(target, weight[2, :, lanes])
            sigmoid = jax.nn.sigmoid(gate)
            active = gate * sigmoid
            product = (active * upward).astype(BF)
            delta_gate = (backward * upward * sigmoid * (1.0 + gate * (1.0 - sigmoid))).astype(BF)
            delta_upper = (backward * active).astype(BF)
            total[0, :, lanes] += dot_tn(delta_gate, key_part)
            total[1, :, lanes] += dot_tn(delta_upper, key_part)
            total[2, :, lanes] += dot_tn(product, target)

    wait_all(small.at[pl.ds(0, count - 1)], small_recv)
    arrive(planes[3], 1)
    arrive(planes[2], 0)
    load.wait()
    near = hd // 2 * 2 * segs
    learn(near, 2 * segs)
    for order, plane in enumerate(planes):
        send_queries(plane, 1 if order == 3 else 0)
    arrive(planes[1], 0)
    arrive(planes[0], 0)
    learn(2 * segs - near, 2 * segs)

    theirs = pl.ds(pl.multiple_of((1 - core) * side, 16), side)
    part[...] = total[:, theirs, :].astype(BF)
    swap = remote(part, half_in, core_send, core_recv, partner)
    swap.start()
    swap.wait_recv()

    def fold(step, carry):
        spot = (chip + 1 + step) % chips
        mine = pl.ds(pl.multiple_of(core * side + spot * rows, 16), rows)
        theirs = pl.ds(pl.multiple_of(spot * rows, 16), rows)
        half[spot] = (total[:, mine, :] + half_in[:, theirs, :].astype(F32)).astype(BF)

        @pl.when(step < chips - 1)
        def _():
            there = hd * segs + spot * 2 + core
            remote(half.at[spot], slices.at[chip], cut_send, cut_recv.at[chip], there).start()

        return carry

    lax.fori_loop(0, chips, fold, 0)

    wait_all(kv.at[0], next_recv)
    wait_all(kv.at[2], prev_recv)

    def order_of(index):
        spot = pick_column(index, 0, count, heads)
        down, across = iota((tokens, tokens), 0), iota((tokens, tokens), 1)
        row = jnp.sum(jnp.where(down == across, spot, 0.0), axis=0, keepdims=True)
        return jnp.where((down + index * tokens).astype(F32) == row, 1.0, 0.0).astype(BF)

    for which, index in enumerate(((seg + segs - 1) % segs, seg, (seg + 1) % segs)):
        sort = order_of(index)
        keys = kv[which, :, 0:home, :].reshape(tokens, width)
        values = kv[which, :, home : 2 * home, :].reshape(tokens, width)
        ahead[0, which * tokens : (which + 1) * tokens, :] = dot_nn(sort, keys).astype(BF)
        ahead[1, which * tokens : (which + 1) * tokens, :] = dot_nn(sort, values).astype(BF)
        if which == 1:
            wait_all(queries.at[pl.ds(0, count - 1)], q_recv)
            sorted_q[...] = dot_nn(sort, queries[...].reshape(tokens, width)).astype(BF)

    reach = WINDOW // 2
    chunk = LANES
    wide = chunk + 2 * reach
    blocks = tokens // chunk
    id_rows = ids_ref.shape[0]
    down, across = iota((chunk, chunk), 0), iota((chunk, chunk), 1)
    for part_index in range(blocks):
        middle = seg * blocks + part_index
        mine = ids_ref[pl.ds(middle, 1), :]
        mine = jnp.sum(jnp.where(down == across, mine, 0), axis=1, keepdims=True)
        for tile in range(wide // chunk):
            block = middle - reach // chunk + tile
            valid = (block >= 0) & (block < id_rows)
            other = ids_ref[pl.ds((block + id_rows) % id_rows, 1), :]
            other = jnp.where(valid, other, -1)
            distance = down - across + (reach - tile * chunk)
            allowed = (mine == other) & (distance < reach) & (distance > -reach)
            bias[part_index, :, tile * chunk : (tile + 1) * chunk] = jnp.where(
                allowed, 0.0, -1e30
            )

    def attend(head, carry):
        lanes = pl.ds(pl.multiple_of(head * ATT_DIM, LANES), ATT_DIM)
        for part_index in range(blocks):
            begin = part_index * chunk
            query = sorted_q[begin : begin + chunk, lanes]
            keys = ahead[0, begin : begin + wide, lanes]
            values = ahead[1, begin : begin + wide, lanes]
            scores = dot_nt(query, keys) * ATT_DIM ** (-0.5) + bias[part_index]
            peak = jnp.max(scores, axis=1, keepdims=True)
            weights = jnp.exp(scores - peak)
            norm = jnp.sum(weights, axis=1, keepdims=True)
            combined[begin : begin + chunk, lanes] = dot_nn(weights.astype(BF), values) / norm
        return carry

    def cut_arrive(step, carry):
        source = (chip + step) % chips
        block = slices.at[source]
        remote(block, block, cut_send, cut_recv.at[source], me).wait_recv()
        return carry

    early = width // ATT_DIM // 2
    lax.fori_loop(0, early, attend, 0)

    lax.fori_loop(1, chips, cut_arrive, 0)
    slices[chip] = half[chip]
    slot = core * chips + chip
    mine = pl.ds(pl.multiple_of(slot * rows, 16), rows)
    for matrix in range(3):
        base = weight[matrix, mine, :].astype(F32)
        update = base + jnp.sum(slices[:, matrix].astype(F32), axis=0)
        scaling = jnp.zeros_like(update)
        for which in range(heads):
            inside = (column >= which * head_dim) & (column < (which + 1) * head_dim)
            old = jnp.sum(jnp.where(inside, base * base, 0.0), axis=1, keepdims=True)
            new = jnp.sum(jnp.where(inside, update * update, 0.0), axis=1, keepdims=True)
            ratio = jnp.sqrt(old + epsilon) / jnp.sqrt(new + epsilon)
            scaling = jnp.where(inside, ratio, scaling)
        fresh[slot, matrix] = (update * scaling).astype(BF)

    def share(step, carry):
        spot = (chip + step) % chips
        there = hd * segs + spot * 2 + core
        remote(fresh.at[slot], fresh.at[slot], share_send, share_recv.at[chip], there).start()
        return carry

    lax.fori_loop(1, chips, share, 0)

    def hand(index):
        remote(fresh.at[index], fresh.at[index], pass_send, pass_recv, partner).start()

    hand(slot)
    lax.fori_loop(early, width // ATT_DIM, attend, 0)

    def shared(step, carry):
        source = (chip + step) % chips
        block = fresh.at[core * chips + source]
        remote(block, block, share_send, share_recv.at[source], me).wait_recv()
        hand(core * chips + source)
        return carry

    lax.fori_loop(1, chips, shared, 0)
    wait_all(fresh.at[pl.ds(0, chips)], pass_recv)

    for which in range(heads):
        lanes, inside = span(which)
        query = jnp.where(inside, sorted_q[:, lanes].astype(F32), 0.0).astype(BF)

        def matrix_of(matrix):
            return fresh[:, matrix, :, lanes].reshape(hidden, -1)

        gate = dot_nt(query, matrix_of(0))
        upward = dot_nt(query, matrix_of(1))
        product = (gate * jax.nn.sigmoid(gate) * upward).astype(BF)
        combined[:, lanes] += jnp.where(inside, dot_nn(product, matrix_of(2)), 0.0)

    tok_dev = out_ref.shape[0]
    for piece in range(SPLIT):
        there = seg * SPLIT + piece
        outgoing[piece] = combined[piece * tok_dev : (piece + 1) * tok_dev, :].astype(BF)

        @pl.when(there != me)
        def _():
            remote(
                outgoing.at[piece], returned.at[hd], back_send.at[piece], back_recv.at[hd], there
            ).start()

        @pl.when(there == me)
        def _():
            returned[hd] = outgoing[piece]

    for source in range(SPLIT):
        block = returned.at[source]

        @pl.when(place.rank(source, me // SPLIT) != me)
        def _():
            remote(block, block, back_send.at[0], back_recv.at[source], me).wait_recv()

    square = 0.0
    for source in range(SPLIT):
        piece = returned[source].astype(F32)
        square = square + jnp.sum(piece * piece, axis=1, keepdims=True)
    scale = lax.rsqrt(square / (SPLIT * width) + epsilon)
    for source in range(SPLIT):
        lanes = slice(source * width, (source + 1) * width)
        out_ref[:, lanes] = (returned[source].astype(F32) * scale * gain_ref[:, lanes]).astype(BF)

    wait_all(small.at[pl.ds(0, count - 1)], small_send)
    wait_all(kv.at[1, pl.ds(0, count - 1)], kv_send)
    wait_all(queries.at[pl.ds(0, count - 1)], q_send)
    wait_all(kv.at[0], next_send)
    wait_all(kv.at[2], prev_send)
    swap.wait_send()
    wait_all(slices.at[pl.ds(0, chips - 1)], cut_send)
    wait_all(fresh.at[pl.ds(0, chips - 1)], share_send)
    wait_all(fresh.at[pl.ds(0, chips)], pass_send)
    for piece in range(SPLIT):
        block = outgoing.at[piece]

        @pl.when(seg * SPLIT + piece != me)
        def _():
            remote(block, block, back_send.at[piece], back_recv.at[0], me).wait_send()


def shards(
    queries, key_rows, value_rows, learn_rates, frame_order, window_ids, fast_init, norm_gain
):
    tok_dev, model = queries.shape
    count = lax.axis_size("tok")
    place = Place(count)
    segs, chips = place.segs, place.chips
    assert count % (2 * SPLIT) == 0 and tok_dev % segs == 0
    home = tok_dev // segs
    width = model // SPLIT
    head_dim = model // HEADS
    hidden = fast_init.shape[0]
    tokens = count * home
    assert tokens == WINDOW // 2 and hidden % (2 * chips) == 0
    rows = hidden // (2 * chips)
    blocks = tokens // LANES
    wide = LANES + WINDOW
    order = frame_order.reshape(count, tok_dev)
    ids = window_ids.reshape(-1, LANES)

    kv, own_q, small = pl.pallas_call(
        functools.partial(pack_kernel, segs),
        name="pack",
        out_shape=(
            jax.ShapeDtypeStruct((SPLIT, segs, 2 * home, width), BF),
            jax.ShapeDtypeStruct((SPLIT, segs, home, width), BF),
            jax.ShapeDtypeStruct((SPLIT, 4, tok_dev), F32),
        ),
        grid=(SPLIT,),
        in_specs=[
            pl.BlockSpec(order.shape, lambda h: (0, 0)),
            pl.BlockSpec((HEADS, tok_dev), lambda h: (0, 0)),
            pl.BlockSpec((tok_dev, width), lambda h: (0, h)),
            pl.BlockSpec((tok_dev, width), lambda h: (0, h)),
            pl.BlockSpec((tok_dev, width), lambda h: (0, h)),
        ],
        out_specs=(
            pl.BlockSpec((1, segs, 2 * home, width), lambda h: (h, 0, 0, 0)),
            pl.BlockSpec((1, segs, home, width), lambda h: (h, 0, 0, 0)),
            pl.BlockSpec((SPLIT, 4, tok_dev), lambda h: (0, 0, 0)),
        ),
        compiler_params=pltpu.CompilerParams(vmem_limit_bytes=16 * 1024 * 1024),
        cost_estimate=pl.CostEstimate(
            flops=6 * tok_dev * tok_dev * model,
            bytes_accessed=12 * tok_dev * model,
            transcendentals=0,
        ),
    )(order, learn_rates.T, queries, key_rows, value_rows)

    dma = pltpu.SemaphoreType.DMA
    return pl.pallas_call(
        functools.partial(layer_kernel, place, head_dim),
        name="layer",
        out_shape=jax.ShapeDtypeStruct((tok_dev, model), BF),
        in_specs=[VM, VM, VM, VM, ANY, VM],
        out_specs=VM,
        scratch_shapes=[
            pltpu.VMEM((3, count, 2 * home, width), BF),
            pltpu.VMEM((count, home, width), BF),
            pltpu.VMEM((count, 4, tok_dev), F32),
            pltpu.VMEM((3, hidden, width), BF),
            pltpu.VMEM((3, hidden, width), F32),
            pltpu.VMEM((3, hidden // 2, width), BF),
            pltpu.VMEM((3, hidden // 2, width), BF),
            pltpu.VMEM((chips, 3, rows, width), BF),
            pltpu.VMEM((chips, 3, rows, width), BF),
            pltpu.VMEM((2 * chips, 3, rows, width), BF),
            pltpu.VMEM((2, 3 * tokens, width), BF),
            pltpu.VMEM((tokens, width), BF),
            pltpu.VMEM((blocks, LANES, wide), F32),
            pltpu.VMEM((tokens, width), F32),
            pltpu.VMEM((SPLIT, tok_dev, width), BF),
            pltpu.VMEM((SPLIT, tok_dev, width), BF),
            dma, dma, dma((count,)), dma, dma, dma, dma, dma, dma, dma, dma,
            dma, dma, dma, dma((chips,)), dma, dma((chips,)), dma, dma,
            dma((SPLIT,)), dma((SPLIT,)),
        ],
        compiler_params=pltpu.CompilerParams(
            vmem_limit_bytes=VMEM_BYTES, collective_id=0, has_side_effects=True
        ),
        cost_estimate=pl.CostEstimate(
            flops=60 * tokens * hidden * width, bytes_accessed=20 * tokens * width,
            transcendentals=0,
        ),
    )(kv, own_q, small, ids, fast_init.transpose(1, 0, 2), norm_gain[None, :])


def solution(mesh):
    rows = P(("groups", "tok"), None)
    return jax.shard_map(
        shards,
        mesh=mesh,
        in_specs=(rows, rows, rows, rows, P("groups"), P("groups"), P(), P()),
        out_specs=rows,
        check_vma=False,
    )
```

time: 248 us -> 134 us (0.54)
  the two profiles are of different devices: /device:TPU:0 before, /device:TPU:31 now
where the time goes in v1:
time: 134 us
  Pallas kernels  123 us (92%)
  local copies, waits for them, and re-layouts  10.4 us (8%)
    pallas_call x1, Pallas kernels, shards(): pl.pallas_call(functools.partial(layer_kernel, place, head_dim), name='la...  122 us
    unnamed x17, local copies, waits for them, and re-layouts  9.12 us

profile of v1, /device:TPU:31, one launch (start us, length us, event | category | flops | bytes accessed | tf_op | source)
XLA Modules:
  0.0 133.9 jit_solution(9246767985964927632)
XLA Ops:
  0.0 1.3 broadcast_in_dim.3.gain_ref
  1.3 0.0 copy-start
  1.3 1.1 copy-done
  2.4 0.0 copy-start.1
  2.4 1.1 copy-done.1
  3.5 0.0 copy-start.2
  3.5 1.1 copy-done.2
  4.6 0.0 copy-start.3
  4.6 0.7 copy-done.3
  5.3 0.0 copy-start.4
  5.3 0.7 copy-done.4
  6.0 1.9 %pack.1 = (bf16[4,8,32,640]{3,2,1,0:T(8,128)(2,1)S(1)}, bf16[4,8,16,640]{3,2,1,0:T(8,128)(2,1)S(1)}, f32[4,4,128]{2,1,0:T(4,128)S(1)}) custom-call(s32[32,128]{1,0:T(8,128)S(1)} %bitcast.4, f32[8,128]{1,0:T(8,128)S(1)} %bitcast.5, bf16[128,2560]{1,0:T(8,128)(2,1)S(1)} %copy-done, bf16[128,2560]{1,0:T(8,128)(2,1)S(1)} %copy-done.1, ...), custom_call_target="tpu_custom_call" | custom-call | flops 251658240 | bytes 3932160 | tf_op jit(solution)/shard_map/pack/pallas_call | solution.py:456
  7.9 0.0 copy-start.5
  7.9 1.1 copy-done.5
  9.0 0.0 copy-start.6
  9.0 0.8 copy-done.6
  9.8 0.0 copy-start.7
  9.8 0.6 copy-done.7
  10.4 121.5 %layer.1 = bf16[128,2560]{1,0:T(8,128)(2,1)} custom-call(bf16[4,8,32,640]{3,2,1,0:T(8,128)(2,1)} %copy-done.5, bf16[4,8,16,640]{3,2,1,0:T(8,128)(2,1)} %copy-done.6, f32[4,4,128]{2,1,0:T(4,128)} %copy-done.7, s32[32,128]{1,0:T(8,128)} %bitcast.7, bf16[3,640,2560]{2,1,0:T(8,128)(2,1)} %bitcast.6, f32[1,2560]{1,0:T(1,128)} %broadcast_in_dim.3.gain_ref), custom_call_target="tpu_custom_call" | custom-call | flops 12582912000 | bytes 6553600 | tf_op jit(solution)/shard_map/layer/pallas_call | solution.py:486
  131.9 2.0 %copy.10 = bf16[128,2560]{1,0:T(8,128)(2,1)} copy(bf16[128,2560]{1,0:T(8,128)(2,1)} %layer.1) | data formatting | bytes 1310720
Async XLA Ops:
  1.3 1.1 copy-start
  2.4 1.1 copy-start.1
  3.5 1.1 copy-start.2
  4.6 0.7 copy-start.3
  5.3 0.7 copy-start.4
  7.9 1.1 copy-start.5
  9.0 0.8 copy-start.6
  9.8 0.6 copy-start.7

commit v2 on v1

--- a/solution.py
+++ b/solution.py
@@ -67,14 +67,10 @@
         return hd * self.segs + chip * 2 + core
 
 
-def pack_kernel(segs, order_ref, rate_ref, query_ref, key_ref, value_ref, kv_ref, q_ref, small_ref):
-    me = lax.axis_index("tok")
-    tokens, width = key_ref.shape
-    home = tokens // segs
-    row = order_ref[pl.ds(me, 1), :].astype(F32)
+def ranks_of(row, segs):
+    tokens = row.shape[1]
     down, across = iota((tokens, tokens), 0), iota((tokens, tokens), 1)
-    same = down == across
-    column = jnp.sum(jnp.where(same, row, 0.0), axis=1, keepdims=True)
+    column = jnp.sum(jnp.where(down == across, row, 0.0), axis=1, keepdims=True)
     span = 1.0 / (SPLIT * tokens)
 
     def sort_key(place, index):
@@ -85,30 +81,16 @@
     rank_row = jnp.sum(jnp.where(key_column < key_row, 1.0, 0.0), axis=0, keepdims=True)
     rank_column = jnp.sum(jnp.where(key_row < key_column, 1.0, 0.0), axis=1, keepdims=True)
     pick = jnp.where(down.astype(F32) == rank_row, 1.0, 0.0).astype(BF)
-    keys = dot_nn(pick, key_ref[...]).astype(BF)
-    values = dot_nn(pick, value_ref[...]).astype(BF)
-    rows = dot_nn(pick, query_ref[...]).astype(BF)
-    kv_ref[0, :, 0:home, :] = keys.reshape(segs, home, width)
-    kv_ref[0, :, home : 2 * home, :] = values.reshape(segs, home, width)
-    q_ref[0] = rows.reshape(segs, home, width)
-
-    @pl.when(pl.program_id(0) == 0)
-    def _():
-        put = jnp.where(across.astype(F32) == rank_column, 1.0, 0.0)
-        place = jnp.sum(put * column, axis=0, keepdims=True)
-        rates = jnp.dot(rate_ref[...], put, precision=lax.Precision.HIGHEST)
-        heads = HEADS // SPLIT
-        for hd in range(SPLIT):
-            small_ref[hd, 0:heads, :] = rates[hd * heads : (hd + 1) * heads]
-            small_ref[hd, heads : heads + 1, :] = place
-            small_ref[hd, heads + 1 :, :] = jnp.zeros_like(small_ref[hd, heads + 1 :, :])
+    put = jnp.where(across.astype(F32) == rank_column, 1.0, 0.0)
+    return pick, put, column
 
 
 def layer_kernel(
-    place, head_dim, kv_ref, q_ref, small_ref, ids_ref, init_ref, gain_ref, out_ref,
-    kv, queries, small, weight, total, part, half_in, half, slices, fresh, ahead, sorted_q,
+    place, head_dim, query_hbm, key_hbm, value_hbm, rate_hbm, order_hbm, ids_hbm, init_ref,
+    gain_hbm, out_ref,
+    stored, rate_ref, order_ref, ids_ref, gain_ref, kv_ref, q_ref, small_ref, kv, queries, small, weight, total, part, half_in, half, slices, fresh, ahead, sorted_q,
     bias, combined, outgoing, returned,
-    init_sem, kv_send, kv_recv, q_send, q_recv, small_send, small_recv, next_send, next_recv,
+    load_sem, init_sem, kv_send, kv_recv, q_send, q_recv, small_send, small_recv, next_send, next_recv,
     prev_send, prev_recv, core_send, core_recv, cut_send, cut_recv, share_send, share_recv,
     pass_send, pass_recv, back_send, back_recv,
 ):
@@ -137,9 +119,21 @@
         pltpu.make_async_copy(buffer, buffer, sem).wait()
 
     columns = pl.ds(pl.multiple_of(hd * width, LANES), width)
+
+    loads = [
+        pltpu.make_async_copy(source, target, load_sem.at[index])
+        for index, (source, target) in enumerate(
+            (
+                (order_hbm, order_ref), (key_hbm, stored.at[0]), (value_hbm, stored.at[1]),
+                (rate_hbm, rate_ref), (query_hbm, stored.at[2]), (ids_hbm, ids_ref),
+                (gain_hbm, gain_ref),
+            )
+        )
+    ]
+    for copy in loads:
+        copy.start()
     load = pltpu.make_async_copy(init_ref.at[:, :, columns], weight, init_sem)
     load.start()
-
     barrier = pltpu.get_barrier_semaphore()
 
     def greet(step, carry):
@@ -150,53 +144,100 @@
         return carry
 
     lax.fori_loop(1, count, greet, 0)
+    loads[0].wait()
+    row = order_ref[pl.ds(me, 1), :].astype(F32)
+    pick, put, position = ranks_of(row, segs)
+    loads[3].wait()
+    rates = jnp.dot(rate_ref[...], put, precision=lax.Precision.HIGHEST)
+    position = jnp.sum(put * position, axis=0, keepdims=True)
+    for index in range(SPLIT):
+        small_ref[index, 0:heads, :] = rates[index * heads : (index + 1) * heads]
+        small_ref[index, heads : heads + 1, :] = position
+        small_ref[index, heads + 1 :, :] = jnp.zeros_like(small_ref[index, heads + 1 :, :])
+    loads[1].wait()
+    loads[2].wait()
+    for index in range(SPLIT):
+        lanes = slice(index * width, (index + 1) * width)
+        for which in range(2):
+            picked = dot_nn(pick, stored[which, :, lanes]).astype(BF)
+            kv_ref[index, :, which * home : (which + 1) * home, :] = picked.reshape(
+                segs, home, width
+            )
     pl.semaphore_wait(barrier, count - 1)
 
-    planes = [(hd + 2) % 4, 3 - hd, hd + 1 - 2 * (hd % 2), hd]
-
-    def send_rows(plane, first):
+    pairs = [((hd + 2) % 4, hd), (3 - hd, hd + 1 - 2 * (hd % 2))]
+
+    def send_small(pair, first, last):
+        def body(step, carry):
+            for plane in pair:
+                there = plane * segs + (within + step) % segs
+                remote(small_ref.at[plane], small.at[me], small_send, small_recv, there).start()
+            return carry
+
+        lax.fori_loop(first, last, body, 0)
+
+    def send_rows(pair, first, last):
         def body(step, carry):
             spot = (within + step) % segs
-            there = plane * segs + spot
-            where = place.seg(plane, spot)
-            remote(small_ref.at[plane], small.at[me], small_send, small_recv, there).start()
-            remote(kv_ref.at[plane, where], kv.at[1, me], kv_send, kv_recv.at[me], there).start()
+            for plane in pair:
+                there = plane * segs + spot
+                where = place.seg(plane, spot)
+                remote(
+                    kv_ref.at[plane, where], kv.at[1, me], kv_send, kv_recv.at[me], there
+                ).start()
             return carry
 
-        lax.fori_loop(first, segs, body, 0)
-
-    def send_queries(plane, first):
+        lax.fori_loop(first, last, body, 0)
+
+    def send_queries(pair, first, last):
         def body(step, carry):
             spot = (within + step) % segs
-            there = plane * segs + spot
-            where = place.seg(plane, spot)
-            remote(q_ref.at[plane, where], queries.at[me], q_send, q_recv, there).start()
+            for plane in pair:
+                there = plane * segs + spot
+                where = place.seg(plane, spot)
+                remote(q_ref.at[plane, where], queries.at[me], q_send, q_recv, there).start()
             return carry
 
-        lax.fori_loop(first, segs, body, 0)
-
-    for order, plane in enumerate(planes):
-        send_rows(plane, 1 if order == 3 else 0)
+        lax.fori_loop(first, last, body, 0)
+
+    def each(action):
+        for index, pair in enumerate(pairs):
+            if index == 0:
+                action(pair[:1], 0, 1)
+                action(pair, 1, segs)
+            else:
+                action(pair, 0, segs)
+
+    each(send_small)
+    each(send_rows)
 
     def forward(block, source):
         remote(block, kv.at[0, source], next_send, next_recv, after).start()
         remote(block, kv.at[2, source], prev_send, prev_recv, before).start()
 
+    loads[4].wait()
+    for index in range(SPLIT):
+        lanes = slice(index * width, (index + 1) * width)
+        picked = dot_nn(pick, stored[2, :, lanes]).astype(BF)
+        q_ref[index] = picked.reshape(segs, home, width)
+    loads[5].wait()
+    loads[6].wait()
     own = kv_ref.at[hd, seg]
     forward(own, me)
     kv[1, me] = kv_ref[hd, seg]
     queries[me] = q_ref[hd, seg]
     small[me] = small_ref[hd]
 
-    def arrive(plane, first):
+    def arrive(pair, first, last):
         def body(step, carry):
-            source = plane * segs + (within + segs - step) % segs
-            block = kv.at[1, source]
-            remote(block, block, kv_send, kv_recv.at[source], source).wait_recv()
-            forward(block, source)
+            for plane in pair:
+                source = plane * segs + (within + segs - step) % segs
+                block = kv.at[1, source]
+                remote(block, block, kv_send, kv_recv.at[source], source).wait_recv()
+                forward(block, source)
             return carry
 
-        lax.fori_loop(first, segs, body, 0)
+        lax.fori_loop(first, last, body, 0)
 
     total[...] = jnp.zeros_like(total)
 
@@ -216,13 +257,25 @@
         chosen = jnp.where(lane[None], held[:, None, :], 0.0)
         return jnp.sum(chosen, axis=2, keepdims=True).reshape(sources * home, 1)
 
-    def learn(base, sources):
-        group = sources * home
+    def learn(pair):
+        group = segs * home
         for which in range(heads):
             lanes, inside = span(which)
-            keys = kv[1, pl.ds(base, sources), 0:home, lanes].reshape(group, -1)
-            values = kv[1, pl.ds(base, sources), home : 2 * home, lanes].reshape(group, -1)
-            rate = pick_column(seg, base, sources, which)
+            keys, values, rate = (
+                jnp.concatenate(parts, axis=0)
+                for parts in zip(
+                    *(
+                        (
+                            kv[1, pl.ds(plane * segs, segs), 0:home, lanes].reshape(group, -1),
+                            kv[1, pl.ds(plane * segs, segs), home : 2 * home, lanes].reshape(
+                                group, -1
+                            ),
+                            pick_column(seg, plane * segs, segs, which),
+                        )
+                        for plane in pair
+                    )
+                )
+            )
             key_part = jnp.where(inside, keys.astype(F32), 0.0).astype(BF)
             target = jnp.where(inside, values.astype(F32) * rate, 0.0).astype(BF)
             gate = dot_nt(key_part, weight[0, :, lanes])
@@ -237,17 +290,16 @@
             total[1, :, lanes] += dot_tn(delta_upper, key_part)
             total[2, :, lanes] += dot_tn(product, target)
 
+    arrive(pairs[0][:1], 0, 1)
+    arrive(pairs[0], 1, segs // 2)
+    arrive(pairs[0], segs // 2, segs)
     wait_all(small.at[pl.ds(0, count - 1)], small_recv)
-    arrive(planes[3], 1)
-    arrive(planes[2], 0)
     load.wait()
-    near = hd // 2 * 2 * segs
-    learn(near, 2 * segs)
-    for order, plane in enumerate(planes):
-        send_queries(plane, 1 if order == 3 else 0)
-    arrive(planes[1], 0)
-    arrive(planes[0], 0)
-    learn(2 * segs - near, 2 * segs)
+    learn(pairs[0])
+    each(send_queries)
+    arrive(pairs[1], 0, segs // 2)
+    arrive(pairs[1], segs // 2, segs)
+    learn(pairs[1])
 
     theirs = pl.ds(pl.multiple_of((1 - core) * side, 16), side)
     part[...] = total[:, theirs, :].astype(BF)
@@ -272,7 +324,7 @@
 
     wait_all(kv.at[0], next_recv)
     wait_all(kv.at[2], prev_recv)
-
+    wait_all(queries.at[pl.ds(0, count - 1)], q_recv)
     def order_of(index):
         spot = pick_column(index, 0, count, heads)
         down, across = iota((tokens, tokens), 0), iota((tokens, tokens), 1)
@@ -286,7 +338,6 @@
         ahead[0, which * tokens : (which + 1) * tokens, :] = dot_nn(sort, keys).astype(BF)
         ahead[1, which * tokens : (which + 1) * tokens, :] = dot_nn(sort, values).astype(BF)
         if which == 1:
-            wait_all(queries.at[pl.ds(0, count - 1)], q_recv)
             sorted_q[...] = dot_nn(sort, queries[...].reshape(tokens, width)).astype(BF)
 
     reach = WINDOW // 2
@@ -414,7 +465,12 @@
     scale = lax.rsqrt(square / (SPLIT * width) + epsilon)
     for source in range(SPLIT):
         lanes = slice(source * width, (source + 1) * width)
-        out_ref[:, lanes] = (returned[source].astype(F32) * scale * gain_ref[:, lanes]).astype(BF)
+        gain = [
+            gain_ref[tile : tile + 1, :]
+            for tile in range(source * width // LANES, (source + 1) * width // LANES)
+        ]
+        gain = jnp.concatenate(gain, axis=1)
+        out_ref[:, lanes] = (returned[source].astype(F32) * scale * gain).astype(BF)
 
     wait_all(small.at[pl.ds(0, count - 1)], small_send)
     wait_all(kv.at[1, pl.ds(0, count - 1)], kv_send)
@@ -452,44 +508,24 @@
     wide = LANES + WINDOW
     order = frame_order.reshape(count, tok_dev)
     ids = window_ids.reshape(-1, LANES)
-
-    kv, own_q, small = pl.pallas_call(
-        functools.partial(pack_kernel, segs),
-        name="pack",
-        out_shape=(
-            jax.ShapeDtypeStruct((SPLIT, segs, 2 * home, width), BF),
-            jax.ShapeDtypeStruct((SPLIT, segs, home, width), BF),
-            jax.ShapeDtypeStruct((SPLIT, 4, tok_dev), F32),
-        ),
-        grid=(SPLIT,),
-        in_specs=[
-            pl.BlockSpec(order.shape, lambda h: (0, 0)),
-            pl.BlockSpec((HEADS, tok_dev), lambda h: (0, 0)),
-            pl.BlockSpec((tok_dev, width), lambda h: (0, h)),
-            pl.BlockSpec((tok_dev, width), lambda h: (0, h)),
-            pl.BlockSpec((tok_dev, width), lambda h: (0, h)),
-        ],
-        out_specs=(
-            pl.BlockSpec((1, segs, 2 * home, width), lambda h: (h, 0, 0, 0)),
-            pl.BlockSpec((1, segs, home, width), lambda h: (h, 0, 0, 0)),
-            pl.BlockSpec((SPLIT, 4, tok_dev), lambda h: (0, 0, 0)),
-        ),
-        compiler_params=pltpu.CompilerParams(vmem_limit_bytes=16 * 1024 * 1024),
-        cost_estimate=pl.CostEstimate(
-            flops=6 * tok_dev * tok_dev * model,
-            bytes_accessed=12 * tok_dev * model,
-            transcendentals=0,
-        ),
-    )(order, learn_rates.T, queries, key_rows, value_rows)
+    gain = norm_gain.reshape(-1, LANES)
 
     dma = pltpu.SemaphoreType.DMA
     return pl.pallas_call(
         functools.partial(layer_kernel, place, head_dim),
         name="layer",
         out_shape=jax.ShapeDtypeStruct((tok_dev, model), BF),
-        in_specs=[VM, VM, VM, VM, ANY, VM],
+        in_specs=[ANY] * 8,
         out_specs=VM,
         scratch_shapes=[
+            pltpu.VMEM((3, tok_dev, model), BF),
+            pltpu.VMEM((HEADS, tok_dev), F32),
+            pltpu.VMEM(order.shape, I32),
+            pltpu.VMEM(ids.shape, I32),
+            pltpu.VMEM(gain.shape, F32),
+            pltpu.VMEM((SPLIT, segs, 2 * home, width), BF),
+            pltpu.VMEM((SPLIT, segs, home, width), BF),
+            pltpu.VMEM((SPLIT, 4, tok_dev), F32),
             pltpu.VMEM((3, count, 2 * home, width), BF),
             pltpu.VMEM((count, home, width), BF),
             pltpu.VMEM((count, 4, tok_dev), F32),
@@ -506,7 +542,7 @@
             pltpu.VMEM((tokens, width), F32),
             pltpu.VMEM((SPLIT, tok_dev, width), BF),
             pltpu.VMEM((SPLIT, tok_dev, width), BF),
-            dma, dma, dma((count,)), dma, dma, dma, dma, dma, dma, dma, dma,
+            dma((7,)), dma, dma, dma((count,)), dma, dma, dma, dma, dma, dma, dma, dma,
             dma, dma, dma, dma((chips,)), dma, dma((chips,)), dma, dma,
             dma((SPLIT,)), dma((SPLIT,)),
         ],
@@ -517,7 +553,10 @@
             flops=60 * tokens * hidden * width, bytes_accessed=20 * tokens * width,
             transcendentals=0,
         ),
-    )(kv, own_q, small, ids, fast_init.transpose(1, 0, 2), norm_gain[None, :])
+    )(
+        queries, key_rows, value_rows, learn_rates.T, order, ids,
+        fast_init.transpose(1, 0, 2), gain,
+    )
 
 
 def solution(mesh):

time: 134 us -> 102 us (0.76)
  Pallas kernels: 123 us -> 99.8 us
  local copies, waits for them, and re-layouts: 10.4 us -> 1.97 us
    pallas_call x1, Pallas kernels: 122 us -> 99.8 us  [shards(): pl.pallas_call(functools.partial(layer_kernel, place, head_dim), name='la...]
    unnamed x17 -> x1, local copies, waits for them, and re-layouts: 9.12 us -> 1.97 us
    pallas_call x1 -> x0, Pallas kernels: 1.92 us -> none  [shards(): pl.pallas_call(functools.partial(pack_kernel, segs), name='pack', out_sha...]
where the time goes in v2:
time: 102 us
  Pallas kernels  99.8 us (98%)
  local copies, waits for them, and re-layouts  1.97 us (2%)
    pallas_call x1, Pallas kernels, shards(): pl.pallas_call(functools.partial(layer_kernel, place, head_dim), name='la...  99.8 us

profile of v2, /device:TPU:31, one launch (start us, length us, event | category | flops | bytes accessed | tf_op | source)
XLA Modules:
  0.0 101.8 jit_solution(14541161824295098428)
XLA Ops:
  0.0 99.8 %layer.1 = bf16[128,2560]{1,0:T(8,128)(2,1)} custom-call(bf16[128,2560]{1,0:T(8,128)(2,1)} %query_hbm.1, bf16[128,2560]{1,0:T(8,128)(2,1)} %key_hbm.1, bf16[128,2560]{1,0:T(8,128)(2,1)} %value_hbm.1, f32[8,128]{1,0:T(8,128)} %bitcast.9, s32[32,128]{1,0:T(8,128)} %bitcast.6, s32[32,128]{1,0:T(8,128)} %bitcast.7, bf16[3,640,2560]{2,1,0:T(8,128)(2,1)} %bitcast.5, ...), custom_call_target="tpu_custom_call" | custom-call | flops 12582912000 | bytes 6553600 | tf_op jit(solution)/shard_map/layer/pallas_call | solution.py:514
  99.8 2.0 %copy.10 = bf16[128,2560]{1,0:T(8,128)(2,1)} copy(bf16[128,2560]{1,0:T(8,128)(2,1)} %layer.1) | data formatting | bytes 1310720

commit v3 on v2

--- a/solution.py
+++ b/solution.py
@@ -89,9 +89,9 @@
     place, head_dim, query_hbm, key_hbm, value_hbm, rate_hbm, order_hbm, ids_hbm, init_ref,
     gain_hbm, out_ref,
     stored, rate_ref, order_ref, ids_ref, gain_ref, kv_ref, q_ref, small_ref, kv, queries, small, weight, total, part, half_in, half, slices, fresh, ahead, sorted_q,
-    bias, combined, outgoing, returned,
+    bias, combined, products, outgoing, returned,
     load_sem, init_sem, kv_send, kv_recv, q_send, q_recv, small_send, small_recv, next_send, next_recv,
-    prev_send, prev_recv, core_send, core_recv, cut_send, cut_recv, share_send, share_recv,
+    prev_send, prev_recv, core_send, core_recv, cut_send, cut_recv, relay_send, share_send, share_recv,
     pass_send, pass_recv, back_send, back_recv,
 ):
     me = lax.axis_index("tok")
@@ -165,51 +165,54 @@
             )
     pl.semaphore_wait(barrier, count - 1)
 
-    pairs = [((hd + 2) % 4, hd), (3 - hd, hd + 1 - 2 * (hd % 2))]
-
-    def send_small(pair, first, last):
+    across, mirror, sibling = (hd + 2) % SPLIT, SPLIT - 1 - hd, hd + 1 - 2 * (hd % 2)
+    outer = 1 - (hd + 1) // 2 % 2
+
+    def choose(first, second):
+        return second + outer * (first - second)
+
+    ahead_of = (
+        (choose(across, hd), choose(mirror, sibling)),
+        (choose(hd, across), choose(sibling, mirror)),
+    )
+    expected = (
+        (choose(mirror, across), choose(sibling, hd)),
+        (choose(across, mirror), choose(hd, sibling)),
+    )
+
+    def send_small(plane, step):
+        there = plane * segs + (within + step) % segs
+        remote(small_ref.at[plane], small.at[me], small_send, small_recv, there).start()
+
+    def send_rows(plane, step):
+        spot = (within + step) % segs
+        remote(
+            kv_ref.at[plane, place.seg(plane, spot)], kv.at[1, me], kv_send, kv_recv.at[me],
+            plane * segs + spot,
+        ).start()
+
+    def send_queries(plane, step):
+        spot = (within + step) % segs
+        remote(
+            q_ref.at[plane, place.seg(plane, spot)], queries.at[me], q_send, q_recv,
+            plane * segs + spot,
+        ).start()
+
+    def others(action, group):
         def body(step, carry):
-            for plane in pair:
-                there = plane * segs + (within + step) % segs
-                remote(small_ref.at[plane], small.at[me], small_send, small_recv, there).start()
+            for plane in group:
+
+                @pl.when(plane * segs + step != hd * segs)
+                def _():
+                    action(plane, step)
+
             return carry
 
-        lax.fori_loop(first, last, body, 0)
-
-    def send_rows(pair, first, last):
-        def body(step, carry):
-            spot = (within + step) % segs
-            for plane in pair:
-                there = plane * segs + spot
-                where = place.seg(plane, spot)
-                remote(
-                    kv_ref.at[plane, where], kv.at[1, me], kv_send, kv_recv.at[me], there
-                ).start()
-            return carry
-
-        lax.fori_loop(first, last, body, 0)
-
-    def send_queries(pair, first, last):
-        def body(step, carry):
-            spot = (within + step) % segs
-            for plane in pair:
-                there = plane * segs + spot
-                where = place.seg(plane, spot)
-                remote(q_ref.at[plane, where], queries.at[me], q_send, q_recv, there).start()
-            return carry
-
-        lax.fori_loop(first, last, body, 0)
-
-    def each(action):
-        for index, pair in enumerate(pairs):
-            if index == 0:
-                action(pair[:1], 0, 1)
-                action(pair, 1, segs)
-            else:
-                action(pair, 0, segs)
-
-    each(send_small)
-    each(send_rows)
+        lax.fori_loop(0, segs, body, 0)
+
+    for action in (send_small, send_rows):
+        for group in ahead_of:
+            others(action, group)
 
     def forward(block, source):
         remote(block, kv.at[0, source], next_send, next_recv, after).start()
@@ -228,16 +231,11 @@
     queries[me] = q_ref[hd, seg]
     small[me] = small_ref[hd]
 
-    def arrive(pair, first, last):
-        def body(step, carry):
-            for plane in pair:
-                source = plane * segs + (within + segs - step) % segs
-                block = kv.at[1, source]
-                remote(block, block, kv_send, kv_recv.at[source], source).wait_recv()
-                forward(block, source)
-            return carry
-
-        lax.fori_loop(first, last, body, 0)
+    def arrive(plane, step):
+        source = plane * segs + (within + segs - step) % segs
+        block = kv.at[1, source]
+        remote(block, block, kv_send, kv_recv.at[source], source).wait_recv()
+        forward(block, source)
 
     total[...] = jnp.zeros_like(total)
 
@@ -257,25 +255,26 @@
         chosen = jnp.where(lane[None], held[:, None, :], 0.0)
         return jnp.sum(chosen, axis=2, keepdims=True).reshape(sources * home, 1)
 
-    def learn(pair):
-        group = segs * home
+    theirs = pl.ds(pl.multiple_of((1 - core) * side, 16), side)
+    swaps = [
+        remote(part.at[m], half_in.at[m], core_send.at[m], core_recv.at[m], partner)
+        for m in range(3)
+    ]
+
+    def learn(group, swaps):
+        sources = [
+            plane * segs + (within + segs - step) % segs
+            for plane in group
+            for step in range(segs)
+        ]
+        terms = []
         for which in range(heads):
             lanes, inside = span(which)
-            keys, values, rate = (
-                jnp.concatenate(parts, axis=0)
-                for parts in zip(
-                    *(
-                        (
-                            kv[1, pl.ds(plane * segs, segs), 0:home, lanes].reshape(group, -1),
-                            kv[1, pl.ds(plane * segs, segs), home : 2 * home, lanes].reshape(
-                                group, -1
-                            ),
-                            pick_column(seg, plane * segs, segs, which),
-                        )
-                        for plane in pair
-                    )
-                )
+            keys = jnp.concatenate([kv[1, source, 0:home, lanes] for source in sources], axis=0)
+            values = jnp.concatenate(
+                [kv[1, source, home : 2 * home, lanes] for source in sources], axis=0
             )
+            rate = jnp.concatenate([pick_column(seg, source, 1, which) for source in sources], axis=0)
             key_part = jnp.where(inside, keys.astype(F32), 0.0).astype(BF)
             target = jnp.where(inside, values.astype(F32) * rate, 0.0).astype(BF)
             gate = dot_nt(key_part, weight[0, :, lanes])
@@ -286,59 +285,16 @@
             product = (active * upward).astype(BF)
             delta_gate = (backward * upward * sigmoid * (1.0 + gate * (1.0 - sigmoid))).astype(BF)
             delta_upper = (backward * active).astype(BF)
-            total[0, :, lanes] += dot_tn(delta_gate, key_part)
-            total[1, :, lanes] += dot_tn(delta_upper, key_part)
-            total[2, :, lanes] += dot_tn(product, target)
-
-    arrive(pairs[0][:1], 0, 1)
-    arrive(pairs[0], 1, segs // 2)
-    arrive(pairs[0], segs // 2, segs)
-    wait_all(small.at[pl.ds(0, count - 1)], small_recv)
-    load.wait()
-    learn(pairs[0])
-    each(send_queries)
-    arrive(pairs[1], 0, segs // 2)
-    arrive(pairs[1], segs // 2, segs)
-    learn(pairs[1])
-
-    theirs = pl.ds(pl.multiple_of((1 - core) * side, 16), side)
-    part[...] = total[:, theirs, :].astype(BF)
-    swap = remote(part, half_in, core_send, core_recv, partner)
-    swap.start()
-    swap.wait_recv()
-
-    def fold(step, carry):
-        spot = (chip + 1 + step) % chips
-        mine = pl.ds(pl.multiple_of(core * side + spot * rows, 16), rows)
-        theirs = pl.ds(pl.multiple_of(spot * rows, 16), rows)
-        half[spot] = (total[:, mine, :] + half_in[:, theirs, :].astype(F32)).astype(BF)
-
-        @pl.when(step < chips - 1)
-        def _():
-            there = hd * segs + spot * 2 + core
-            remote(half.at[spot], slices.at[chip], cut_send, cut_recv.at[chip], there).start()
-
-        return carry
-
-    lax.fori_loop(0, chips, fold, 0)
-
-    wait_all(kv.at[0], next_recv)
-    wait_all(kv.at[2], prev_recv)
-    wait_all(queries.at[pl.ds(0, count - 1)], q_recv)
-    def order_of(index):
-        spot = pick_column(index, 0, count, heads)
-        down, across = iota((tokens, tokens), 0), iota((tokens, tokens), 1)
-        row = jnp.sum(jnp.where(down == across, spot, 0.0), axis=0, keepdims=True)
-        return jnp.where((down + index * tokens).astype(F32) == row, 1.0, 0.0).astype(BF)
-
-    for which, index in enumerate(((seg + segs - 1) % segs, seg, (seg + 1) % segs)):
-        sort = order_of(index)
-        keys = kv[which, :, 0:home, :].reshape(tokens, width)
-        values = kv[which, :, home : 2 * home, :].reshape(tokens, width)
-        ahead[0, which * tokens : (which + 1) * tokens, :] = dot_nn(sort, keys).astype(BF)
-        ahead[1, which * tokens : (which + 1) * tokens, :] = dot_nn(sort, values).astype(BF)
-        if which == 1:
-            sorted_q[...] = dot_nn(sort, queries[...].reshape(tokens, width)).astype(BF)
+            terms.append(
+                (lanes, (delta_gate, key_part), (delta_upper, key_part), (product, target))
+            )
+        for matrix in range(3):
+            for term in terms:
+                left, right = term[1 + matrix]
+                total[matrix, :, term[0]] += dot_tn(left, right)
+            if swaps:
+                part[matrix] = total[matrix, theirs, :].astype(BF)
+                swaps[matrix].start()
 
     reach = WINDOW // 2
     chunk = LANES
@@ -360,6 +316,123 @@
             bias[part_index, :, tile * chunk : (tile + 1) * chunk] = jnp.where(
                 allowed, 0.0, -1e30
             )
+    others(arrive, expected[0])
+    wait_all(small.at[pl.ds(0, count - 1)], small_recv)
+    load.wait()
+    learn(expected[0], [])
+
+    def all_queries():
+        for group in ahead_of:
+            others(send_queries, group)
+
+    pl.when(outer == 0)(all_queries)
+    others(arrive, expected[1])
+    learn(expected[1], swaps)
+
+    assert chips == 4
+    flip, turn, corner = chip + 1 - 2 * (chip % 2), (chip + 2) % chips, chips - 1 - chip
+    first_peer = flip + core * (turn - flip)
+    second_peer = turn + core * (flip - turn)
+
+    def on(spot):
+        return hd * segs + spot * 2 + core
+
+    def fold(matrix):
+        def body(spot, carry):
+            mine = pl.ds(pl.multiple_of(core * side + spot * rows, 16), rows)
+            theirs = pl.ds(pl.multiple_of(spot * rows, 16), rows)
+            half[matrix, spot] = (
+                total[matrix, mine, :] + half_in[matrix, theirs, :].astype(F32)
+            ).astype(BF)
+            return carry
+
+        lax.fori_loop(0, chips, body, 0)
+        for index, spot in enumerate((corner, first_peer)):
+            remote(
+                half.at[matrix, spot], slices.at[matrix, index], cut_send,
+                cut_recv.at[3 * matrix + index], on(first_peer),
+            ).start()
+
+    def landed(matrix, index):
+        block = slices.at[matrix, index]
+        remote(block, block, cut_send, cut_recv.at[3 * matrix + index], me).wait_recv()
+
+    def relay(matrix):
+        landed(matrix, 0)
+        slices[matrix, 3] = (
+            half[matrix, second_peer].astype(F32) + slices[matrix, 0].astype(F32)
+        ).astype(BF)
+        remote(
+            slices.at[matrix, 3], slices.at[matrix, 2], relay_send, cut_recv.at[3 * matrix + 2],
+            on(second_peer),
+        ).start()
+
+    for matrix in range(3):
+        swaps[matrix].wait_recv()
+        fold(matrix)
+    def order_of(index):
+        spot = pick_column(index, 0, count, heads)
+        down, across = iota((tokens, tokens), 0), iota((tokens, tokens), 1)
+        row = jnp.sum(jnp.where(down == across, spot, 0.0), axis=0, keepdims=True)
+        return jnp.where((down + index * tokens).astype(F32) == row, 1.0, 0.0).astype(BF)
+
+    def arrange(which, index):
+        sort = order_of(index)
+        keys = kv[which, :, 0:home, :].reshape(tokens, width)
+        values = kv[which, :, home : 2 * home, :].reshape(tokens, width)
+        ahead[0, which * tokens : (which + 1) * tokens, :] = dot_nn(sort, keys).astype(BF)
+        ahead[1, which * tokens : (which + 1) * tokens, :] = dot_nn(sort, values).astype(BF)
+        return sort
+
+    slot = core * chips + chip
+    mine = pl.ds(pl.multiple_of(slot * rows, 16), rows)
+
+    def hand(matrix, index):
+        block = fresh.at[matrix, index]
+        remote(block, block, pass_send, pass_recv.at[matrix], partner).start()
+
+    def renew(matrix):
+        landed(matrix, 1)
+        landed(matrix, 2)
+        base = weight[matrix, mine, :].astype(F32)
+        update = (
+            base
+            + half[matrix, chip].astype(F32)
+            + slices[matrix, 1].astype(F32)
+            + slices[matrix, 2].astype(F32)
+        )
+        scaling = jnp.zeros_like(update)
+        for which in range(heads):
+            inside = (column >= which * head_dim) & (column < (which + 1) * head_dim)
+            old = jnp.sum(jnp.where(inside, base * base, 0.0), axis=1, keepdims=True)
+            new = jnp.sum(jnp.where(inside, update * update, 0.0), axis=1, keepdims=True)
+            ratio = jnp.sqrt(old + epsilon) / jnp.sqrt(new + epsilon)
+            scaling = jnp.where(inside, ratio, scaling)
+        fresh[matrix, slot] = (update * scaling).astype(BF)
+        share(matrix, chip, second_peer)
+        share(matrix, chip, first_peer)
+        hand(matrix, slot)
+
+    def share(matrix, source, peer):
+        block = fresh.at[matrix, core * chips + source]
+        remote(block, block, share_send, share_recv.at[matrix * chips + source], on(peer)).start()
+
+    def collect(matrix, source):
+        block = fresh.at[matrix, core * chips + source]
+        remote(block, block, share_send, share_recv.at[matrix * chips + source], me).wait_recv()
+
+    def onward(matrix):
+        collect(matrix, second_peer)
+        share(matrix, second_peer, first_peer)
+        hand(matrix, core * chips + second_peer)
+
+    def gather(matrix):
+        for source in (first_peer, corner):
+            collect(matrix, source)
+            hand(matrix, core * chips + source)
+
+    def whole(matrix, lanes):
+        return fresh[matrix, :, :, lanes].reshape(hidden, -1)
 
     def attend(head, carry):
         lanes = pl.ds(pl.multiple_of(head * ATT_DIM, LANES), ATT_DIM)
@@ -375,71 +448,50 @@
             combined[begin : begin + chunk, lanes] = dot_nn(weights.astype(BF), values) / norm
         return carry
 
-    def cut_arrive(step, carry):
-        source = (chip + step) % chips
-        block = slices.at[source]
-        remote(block, block, cut_send, cut_recv.at[source], me).wait_recv()
-        return carry
-
-    early = width // ATT_DIM // 2
-    lax.fori_loop(0, early, attend, 0)
-
-    lax.fori_loop(1, chips, cut_arrive, 0)
-    slices[chip] = half[chip]
-    slot = core * chips + chip
-    mine = pl.ds(pl.multiple_of(slot * rows, 16), rows)
+    wait_all(kv.at[0], next_recv)
+    wait_all(kv.at[2], prev_recv)
+    own_order = arrange(1, seg)
+    arrange(0, (seg + segs - 1) % segs)
     for matrix in range(3):
-        base = weight[matrix, mine, :].astype(F32)
-        update = base + jnp.sum(slices[:, matrix].astype(F32), axis=0)
-        scaling = jnp.zeros_like(update)
-        for which in range(heads):
-            inside = (column >= which * head_dim) & (column < (which + 1) * head_dim)
-            old = jnp.sum(jnp.where(inside, base * base, 0.0), axis=1, keepdims=True)
-            new = jnp.sum(jnp.where(inside, update * update, 0.0), axis=1, keepdims=True)
-            ratio = jnp.sqrt(old + epsilon) / jnp.sqrt(new + epsilon)
-            scaling = jnp.where(inside, ratio, scaling)
-        fresh[slot, matrix] = (update * scaling).astype(BF)
-
-    def share(step, carry):
-        spot = (chip + step) % chips
-        there = hd * segs + spot * 2 + core
-        remote(fresh.at[slot], fresh.at[slot], share_send, share_recv.at[chip], there).start()
-        return carry
-
-    lax.fori_loop(1, chips, share, 0)
-
-    def hand(index):
-        remote(fresh.at[index], fresh.at[index], pass_send, pass_recv, partner).start()
-
-    hand(slot)
-    lax.fori_loop(early, width // ATT_DIM, attend, 0)
-
-    def shared(step, carry):
-        source = (chip + step) % chips
-        block = fresh.at[core * chips + source]
-        remote(block, block, share_send, share_recv.at[source], me).wait_recv()
-        hand(core * chips + source)
-        return carry
-
-    lax.fori_loop(1, chips, shared, 0)
-    wait_all(fresh.at[pl.ds(0, chips)], pass_recv)
-
+        relay(matrix)
+    pl.when(outer == 1)(all_queries)
+    arrange(2, (seg + 1) % segs)
+    attend_heads = width // ATT_DIM
+    first = max(attend_heads - 4, 0)
+    renew(0)
+    renew(1)
+    renew(2)
+    wait_all(queries.at[pl.ds(0, count - 1)], q_recv)
+    sorted_q[...] = dot_nn(own_order, queries[...].reshape(tokens, width)).astype(BF)
+    lax.fori_loop(0, first, attend, 0)
+    onward(0)
+    onward(1)
+    onward(2)
+    lax.fori_loop(first, first + 2, attend, 0)
+    gather(0)
+    lax.fori_loop(first + 2, first + 3, attend, 0)
+    gather(1)
+    lax.fori_loop(first + 3, attend_heads, attend, 0)
+    wait_all(fresh.at[0, pl.ds(0, chips)], pass_recv.at[0])
+    wait_all(fresh.at[1, pl.ds(0, chips)], pass_recv.at[1])
     for which in range(heads):
         lanes, inside = span(which)
         query = jnp.where(inside, sorted_q[:, lanes].astype(F32), 0.0).astype(BF)
-
-        def matrix_of(matrix):
-            return fresh[:, matrix, :, lanes].reshape(hidden, -1)
-
-        gate = dot_nt(query, matrix_of(0))
-        upward = dot_nt(query, matrix_of(1))
-        product = (gate * jax.nn.sigmoid(gate) * upward).astype(BF)
-        combined[:, lanes] += jnp.where(inside, dot_nn(product, matrix_of(2)), 0.0)
-
+        gate = dot_nt(query, whole(0, lanes))
+        upward = dot_nt(query, whole(1, lanes))
+        products[which] = (gate * jax.nn.sigmoid(gate) * upward).astype(BF)
+    gather(2)
+    wait_all(fresh.at[2, pl.ds(0, chips)], pass_recv.at[2])
     tok_dev = out_ref.shape[0]
-    for piece in range(SPLIT):
+    for step in range(SPLIT):
+        piece = (within + hd + step) % SPLIT
         there = seg * SPLIT + piece
-        outgoing[piece] = combined[piece * tok_dev : (piece + 1) * tok_dev, :].astype(BF)
+        stretch = pl.ds(pl.multiple_of(piece * tok_dev, tok_dev), tok_dev)
+        for which in range(heads):
+            lanes, inside = span(which)
+            made = dot_nn(products[which, stretch, :], whole(2, lanes))
+            combined[stretch, lanes] += jnp.where(inside, made, 0.0)
+        outgoing[piece] = combined[stretch, :].astype(BF)
 
         @pl.when(there != me)
         def _():
@@ -477,10 +529,12 @@
     wait_all(queries.at[pl.ds(0, count - 1)], q_send)
     wait_all(kv.at[0], next_send)
     wait_all(kv.at[2], prev_send)
-    swap.wait_send()
-    wait_all(slices.at[pl.ds(0, chips - 1)], cut_send)
-    wait_all(fresh.at[pl.ds(0, chips - 1)], share_send)
-    wait_all(fresh.at[pl.ds(0, chips)], pass_send)
+    for matrix in range(3):
+        swaps[matrix].wait_send()
+    wait_all(slices.at[:, pl.ds(0, 2)], cut_send)
+    wait_all(slices.at[:, 3], relay_send)
+    wait_all(fresh.at[:, pl.ds(0, chips - 1)], share_send)
+    wait_all(fresh.at[:, pl.ds(0, chips)], pass_send)
     for piece in range(SPLIT):
         block = outgoing.at[piece]
 
@@ -533,17 +587,19 @@
             pltpu.VMEM((3, hidden, width), F32),
             pltpu.VMEM((3, hidden // 2, width), BF),
             pltpu.VMEM((3, hidden // 2, width), BF),
-            pltpu.VMEM((chips, 3, rows, width), BF),
-            pltpu.VMEM((chips, 3, rows, width), BF),
-            pltpu.VMEM((2 * chips, 3, rows, width), BF),
+            pltpu.VMEM((3, chips, rows, width), BF),
+            pltpu.VMEM((3, chips, rows, width), BF),
+            pltpu.VMEM((3, 2 * chips, rows, width), BF),
             pltpu.VMEM((2, 3 * tokens, width), BF),
             pltpu.VMEM((tokens, width), BF),
             pltpu.VMEM((blocks, LANES, wide), F32),
             pltpu.VMEM((tokens, width), F32),
+            pltpu.VMEM((HEADS // SPLIT, tokens, hidden), BF),
             pltpu.VMEM((SPLIT, tok_dev, width), BF),
             pltpu.VMEM((SPLIT, tok_dev, width), BF),
             dma((7,)), dma, dma, dma((count,)), dma, dma, dma, dma, dma, dma, dma, dma,
-            dma, dma, dma, dma((chips,)), dma, dma((chips,)), dma, dma,
+            dma((3,)), dma((3,)), dma, dma((9,)), dma, dma,
+            dma((3 * chips,)), dma, dma((3,)),
             dma((SPLIT,)), dma((SPLIT,)),
         ],
         compiler_params=pltpu.CompilerParams(

time: 102 us -> 96.6 us (0.947)
  the two profiles are of different devices: /device:TPU:31 before, /device:TPU:4 now
where the time goes in v3:
time: 96.6 us; the launch traced here: 96.4 us
  Pallas kernels  94.4 us (98%)
  local copies, waits for them, and re-layouts  1.97 us (2%)
    pallas_call x1, Pallas kernels, shards(): pl.pallas_call(functools.partial(layer_kernel, place, head_dim), name='la...  94.4 us
    unnamed x1, local copies, waits for them, and re-layouts  1.97 us

profile of v3, /device:TPU:4, one launch (start us, length us, event | category | flops | bytes accessed | tf_op | source)
XLA Modules:
  0.0 96.4 jit_solution(15356374647367349864)
XLA Ops:
  0.0 94.4 %layer.1 = bf16[128,2560]{1,0:T(8,128)(2,1)} custom-call(bf16[128,2560]{1,0:T(8,128)(2,1)} %query_hbm.1, bf16[128,2560]{1,0:T(8,128)(2,1)} %key_hbm.1, bf16[128,2560]{1,0:T(8,128)(2,1)} %value_hbm.1, f32[8,128]{1,0:T(8,128)} %bitcast.9, s32[32,128]{1,0:T(8,128)} %bitcast.6, s32[32,128]{1,0:T(8,128)} %bitcast.7, bf16[3,640,2560]{2,1,0:T(8,128)(2,1)} %bitcast.5, ...), custom_call_target="tpu_custom_call" | custom-call | flops 12582912000 | bytes 6553600 | tf_op jit(solution)/shard_map/layer/pallas_call | solution.py:568
  94.4 2.0 %copy.10 = bf16[128,2560]{1,0:T(8,128)(2,1)} copy(bf16[128,2560]{1,0:T(8,128)(2,1)} %layer.1) | data formatting | bytes 1310720
